TPU v7x, 512 devices: a 8x2x16 block of a 8x8x16 slice. The times are simulated.
512 devices in a mesh: clip: 2 (over y), seq: 32 (over z, core), head: 8 (over x).
Axes of the slice: x: 8, y: 2, z: 16, core: 2. Of those that a mesh axis runs over, the one named last changes fastest.
The devices are a block of a 8x8x16 slice.
Arguments:
- queries: bfloat16 [32, 32, 16, 3072], P(('clip', 'head'), 'seq'), parts along dimension 0, may hold values from -15 to 15
- attn_keys: bfloat16 [32, 32, 16, 3072], P(('clip', 'head'), 'seq'), parts along dimension 0, may hold values from -5 to 5
- attn_values: bfloat16 [32, 32, 16, 3072], P(('clip', 'head'), 'seq'), parts along dimension 0, may hold values from -5 to 5
- residual: bfloat16 [32, 32, 16, 5120], P(('clip', 'head'), 'seq'), parts along dimension 0, may hold values from -6 to 6
- out_weight: bfloat16 [3072, 5120], P('head', 'seq'), may hold values from -0.109375 to 0.109375
- out_gate: float32 [5120], replicated, may hold values from 0.3 to 3
- head_shift: float32 [5120], replicated, may hold values from -3 to 3
- head_scale: float32 [5120], replicated, may hold values from -1.5 to 1.5
- head_weight: bfloat16 [5120, 64], replicated, may hold values from -0.078125 to 0.078125
- head_bias: float32 [64], replicated, may hold values from -3 to 3
- conv_weight: bfloat16 [3, 3, 3, 16, 384], replicated, may hold values from -0.3125 to 0.3125
- conv_bias: float32 [384], replicated, may hold values from -3 to 3
- norm_gain: float32 [384], replicated, may hold values from 0.5 to 2
Outputs:
- hidden: bfloat16 [32, 32, 16, 5120], P(('clip', 'head'), 'seq'), parts along dimension 0
- features: bfloat16 [32, 64, 32, 384], P(('clip', 'head'), 'seq'), parts along dimension 0
There are 2 independent parts, one for each index of `clip`. A program takes and returns all parts, laid end to end along the dimension named above; an argument that names none is the same for every part. Nothing has to cross between parts.
All inputs are finite; a program needn't handle non-finite values.
Results may differ from a plain program's by a relative error of at most 0.013.
Values may be sent and summed in bfloat16 or wider, within the bound.
A program may use at most 128 MiB of HBM per device.

v0:
```python
import jax
import jax.numpy as jnp
from jax import lax
from jax.sharding import PartitionSpec as P

HEAD_DIM = 128


def side_by_side(arrays, axis, dim, along):
    both = jnp.concatenate(arrays, axis=along)
    whole, at, outs = (lax.all_gather(both, axis, axis=dim, tiled=True), 0, [])
    for a in arrays:
        outs.append(lax.slice_in_dim(whole, at, at + a.shape[along], axis=along))
        at += a.shape[along]
    return tuple(outs)


def from_behind(value, axis, steps):
    count = lax.axis_size(axis)
    first, last = (max(0, -steps), min(count, count - steps))
    return lax.ppermute(value, axis, [(source, source + steps) for source in range(first, last)])


def padded_2(x, sides, width):
    for axis, dim in sides:
        peers, length = (lax.axis_size(axis), x.shape[dim])
        up = [(i, (i + 1) % peers) for i in range(peers - 1)]
        down = [(j, i) for i, j in up]
        last = lax.slice_in_dim(x, length - width, length, axis=dim)
        first = lax.slice_in_dim(x, 0, width, axis=dim)
        before = lax.ppermute(last, axis, up)
        after = lax.ppermute(first, axis, down)
        x = jnp.concatenate([before, x, after], axis=dim)
    return x


def head_latent(hidden, head_shift, head_scale, head_weight, head_bias):
    values = hidden.astype(jnp.float32)
    center = values - jnp.mean(values, -1, keepdims=True)
    spread = jnp.mean(center * center, -1, keepdims=True)
    normed = (center * lax.rsqrt(spread + 1e-06) * (1.0 + head_scale) + head_shift).astype(
        jnp.bfloat16
    )
    flat = normed.reshape(-1, normed.shape[-1])
    latent = (jnp.dot(flat, head_weight, preferred_element_type=jnp.float32) + head_bias).astype(
        jnp.bfloat16
    )
    frames, height, breadth = (hidden.shape[0], hidden.shape[1], hidden.shape[2])
    channels = head_weight.shape[1] // 4
    patches = latent.reshape(frames, height, breadth, 2, 2, channels).transpose(0, 1, 3, 2, 4, 5)
    return patches.reshape(frames, height * 2, breadth * 2, channels)


def convolve(padded, frames, conv_weight, conv_bias, norm_gain):
    height = padded.shape[1] - 2
    breadth = padded.shape[2] - 2
    stacked = jnp.concatenate(
        [
            padded[
                time_off : time_off + frames,
                row_off : row_off + height,
                col_off : col_off + breadth,
            ]
            for time_off in range(3)
            for row_off in range(3)
            for col_off in range(3)
        ],
        -1,
    )
    kernel = conv_weight.reshape(-1, conv_weight.shape[-1])
    linear = (
        jnp.dot(stacked.reshape(-1, stacked.shape[-1]), kernel, preferred_element_type=jnp.float32)
        + conv_bias
    )
    normed = linear * lax.rsqrt(jnp.mean(linear * linear, -1, keepdims=True) + 1e-06) * norm_gain
    return jax.nn.silu(normed).astype(jnp.bfloat16).reshape(frames, height, breadth, -1)


def attend_block(carried, block_keys, block_values, query_heads):
    running, denominator, weighted = carried
    scores = jnp.einsum("hqd,khd->hqk", query_heads, block_keys, preferred_element_type=jnp.float32)
    scores = scores * query_heads.shape[-1] ** (-0.5)
    newmax = jnp.maximum(running, jnp.max(scores, -1))
    factor = jnp.exp(running - newmax)
    weights = jnp.exp(scores - newmax[..., None])
    denominator = denominator * factor + jnp.sum(weights, -1)
    product = jnp.einsum(
        "hqk,khd->hqd",
        weights.astype(jnp.bfloat16),
        block_values,
        preferred_element_type=jnp.float32,
    )
    weighted = weighted * factor[..., None] + product
    return (newmax, denominator, weighted)


def fold_pieces(query_heads, carried, pieces):
    key_piece, value_piece = pieces
    frames, height, breadth = (key_piece.shape[0], key_piece.shape[1], key_piece.shape[2])
    heads_here, head_width = (query_heads.shape[0], query_heads.shape[2])
    group_rows = 4

    def regroup(one_piece):
        shaped = one_piece.reshape(
            frames, height // group_rows, group_rows, breadth, heads_here, head_width
        )
        shaped = shaped.transpose(1, 0, 2, 3, 4, 5)
        return shaped.reshape(
            height // group_rows, frames * group_rows * breadth, heads_here, head_width
        )

    def advance(inner, blocks):
        return (attend_block(inner, blocks[0], blocks[1], query_heads), None)

    carried, _ = lax.scan(advance, carried, (regroup(key_piece), regroup(value_piece)))
    return carried


def on_device(
    queries,
    attn_keys,
    attn_values,
    residual,
    out_weight,
    out_gate,
    head_shift,
    head_scale,
    head_weight,
    head_bias,
    conv_weight,
    conv_bias,
    norm_gain,
):
    head_count = lax.axis_size("head")
    frames_dev = queries.shape[0]
    group_width = queries.shape[3] // head_count
    head_width = HEAD_DIM
    heads_here = group_width // head_width
    local_queries, local_keys, local_values = (
        lax.all_to_all(queries, "head", split_axis=3, concat_axis=0, tiled=True),
        lax.all_to_all(attn_keys, "head", split_axis=3, concat_axis=0, tiled=True),
        lax.all_to_all(attn_values, "head", split_axis=3, concat_axis=0, tiled=True),
    )
    frames_all, height, breadth = (
        local_queries.shape[0],
        local_queries.shape[1],
        local_queries.shape[2],
    )
    count = frames_all * height * breadth
    query_heads = local_queries.reshape(count, heads_here, head_width).transpose(1, 0, 2)
    initial = (
        jnp.full((heads_here, count), -1e30, jnp.float32),
        jnp.zeros((heads_here, count), jnp.float32),
        jnp.zeros((heads_here, count, head_width), jnp.float32),
    )
    carried = fold_pieces(
        query_heads, initial, side_by_side((local_keys, local_values), "seq", 1, 0)
    )
    running, denominator, weighted = carried
    attended = (weighted / denominator[..., None]).astype(jnp.bfloat16)
    attended = attended.transpose(1, 0, 2).reshape(count, group_width)
    partial_value = jnp.dot(
        attended,
        lax.all_gather(out_weight, "seq", axis=1, tiled=True),
        preferred_element_type=jnp.float32,
    )
    partial_value = partial_value.reshape(frames_all, height, breadth, partial_value.shape[-1])
    owned = lax.psum_scatter(
        partial_value.astype(jnp.bfloat16), "head", scatter_dimension=0, tiled=True
    ).astype(jnp.float32)
    hidden = (residual.astype(jnp.float32) + out_gate * owned).astype(jnp.bfloat16)
    own_video = head_latent(hidden, head_shift, head_scale, head_weight, head_bias)
    earlier = from_behind(own_video, "head", 1)
    video = jnp.concatenate([earlier, own_video], 0)
    extended = padded_2(video, (("seq", 1),), 1)
    padded = jnp.pad(extended, ((0, 0), (0, 0), (1, 1), (0, 0)))
    features = convolve(padded, frames_dev, conv_weight, conv_bias, norm_gain)
    return (hidden, features)


def solution(mesh):
    return jax.shard_map(
        on_device,
        mesh=mesh,
        in_specs=(
            P(("clip", "head"), "seq", None, None),
            P(("clip", "head"), "seq", None, None),
            P(("clip", "head"), "seq", None, None),
            P(("clip", "head"), "seq", None, None),
            P("head", "seq"),
            P(),
            P(),
            P(),
            P(),
            P(),
            P(),
            P(),
            P(),
        ),
        out_specs=(P(("clip", "head"), "seq", None, None), P(("clip", "head"), "seq", None, None)),
        check_vma=False,
    )
```

profile of v0, /device:TPU:65, one launch (start us, length us, event | category | flops | bytes accessed | tf_op | source)
XLA Modules:
  0.0 373.8 jit_solution(7709526714468302545)
XLA Ops:
  7.2 3.4 copy.79
  12.8 7.9 %all-to-all-start = ((bf16[8,2,6144]{2,1,0:T(2,128)(2,1)}), bf16[8,2,6144]{2,1,0:T(2,128)(2,1)S(1)}, u32[]{:S(2)}, u32[]{:S(2)}) async-start(bf16[8,2,6144]{2,1,0:T(2,128)(2,1)} %reshape.128), calls=%async_computation | async-start | bytes 393216 | tf_op jit(solution)/shard_map/all_to_all | solution.py:141
  24.8 4.5 %all-to-all-done = bf16[8,2,6144]{2,1,0:T(2,128)(2,1)S(1)} async-done(((bf16[8,2,6144]{2,1,0:T(2,128)(2,1)}), bf16[8,2,6144]{2,1,0:T(2,128)(2,1)S(1)}, u32[]{:S(2)}, u32[]{:S(2)}) %all-to-all-start) | async-done | bytes 196640 | tf_op jit(solution)/shard_map/all_to_all | solution.py:141
  29.3 3.6 all-to-all-start.1
  35.1 6.2 %all-to-all-done.1 = bf16[8,2,6144]{2,1,0:T(2,128)(2,1)S(1)} async-done(((bf16[8,2,6144]{2,1,0:T(2,128)(2,1)}), bf16[8,2,6144]{2,1,0:T(2,128)(2,1)S(1)}, u32[]{:S(2)}, u32[]{:S(2)}) %all-to-all-start.1) | async-done | bytes 196640 | tf_op jit(solution)/shard_map/all_to_all | solution.py:142
  48.4 3.6 all-to-all-start.2
  53.1 7.3 %all-to-all-done.2 = bf16[8,2,6144]{2,1,0:T(2,128)(2,1)S(1)} async-done(((bf16[8,2,6144]{2,1,0:T(2,128)(2,1)}), bf16[8,2,6144]{2,1,0:T(2,128)(2,1)S(1)}, u32[]{:S(2)}, u32[]{:S(2)}) %all-to-all-start.2) | async-done | bytes 196640 | tf_op jit(solution)/shard_map/all_to_all | solution.py:140
  62.6 102.7 %all-gather.3.cloned.1.call-done = bf16[32,32,16,384]{3,2,0,1:T(8,128)(2,1)} async-done(((bf16[32,1,16,384]{3,2,0,1:T(8,128)(2,1)}), bf16[32,32,16,384]{3,2,0,1:T(8,128)(2,1)}) %all-gather.3.cloned.1.call-update) | async-done | bytes 12582928 | tf_op jit(solution)/shard_map/all_gather | solution.py:11
  165.2 9.5 %fusion.35 = (bf16[16,32,16,384]{3,2,0,1:T(8,128)(2,1)S(1)}, bf16[16,32,16,384]{3,2,0,1:T(8,128)(2,1)}) fusion(bf16[32,32,16,384]{3,2,0,1:T(8,128)(2,1)} %all-gather.3.cloned.1.call-done), kind=kLoop, calls=%fused_computation.63 | loop fusion | bytes 25165824 | tf_op jit(solution)/shard_map/slice | solution.py:13
  174.7 3.7 copy.90
  178.4 16.8 %reshape.118 = bf16[16,8,4,16,3,128]{5,4,3,2,1,0:T(4,128)(2,1)} reshape(bf16[16,32,16,384]{3,2,1,0:T(8,128)(2,1)} %copy.90) | data formatting | bytes 12582912 | tf_op jit(solution)/shard_map/reshape | solution.py:104
  195.2 8.1 %copy.91 = bf16[8,16,4,16,3,128]{5,3,2,1,4,0:T(8,128)(2,1)} copy(bf16[8,16,4,16,3,128]{5,4,3,2,0,1:T(4,128)(2,1)} %bitcast.110) | data formatting | bytes 12582912 | tf_op jit(solution)/shard_map/transpose | solution.py:107
  203.3 3.5 copy.85
  206.9 16.8 %reshape.115 = bf16[16,8,4,16,3,128]{5,4,3,2,1,0:T(4,128)(2,1)} reshape(bf16[16,32,16,384]{3,2,1,0:T(8,128)(2,1)} %copy.85) | data formatting | bytes 12582912 | tf_op jit(solution)/shard_map/reshape | solution.py:104
  223.6 7.8 %copy.86 = bf16[8,16,4,16,3,128]{5,3,2,1,4,0:T(8,128)(2,1)} copy(bf16[8,16,4,16,3,128]{5,4,3,2,0,1:T(4,128)(2,1)} %bitcast.111) | data formatting | bytes 12582912 | tf_op jit(solution)/shard_map/transpose | solution.py:107
  231.4 66.1 %while.15 = (s32[]{:T(128)}, f32[3,256]{1,0:T(4,128)S(1)}, f32[3,256]{1,0:T(4,128)S(1)}, f32[3,256,128]{2,1,0:T(8,128)S(1)}, bf16[8,1024,3,128]{3,1,2,0:T(8,128)...) while((s32[]{:T(128)}, f32[3,256]{1,0:T(4,128)S(1)}, ...), condition=%wide.region_3.4_spmd.clone, body=%wide.region_0.3_spmd.clone.sunk | while | flops 409243392 | bytes 24626308 | solution.py:115
  239.7 3.3 bitcast_reduce_fusion.2
  248.0 3.3 bitcast_reduce_fusion.2
  256.2 3.3 bitcast_reduce_fusion.2
  264.5 3.3 bitcast_reduce_fusion.2
  272.8 3.3 bitcast_reduce_fusion.2
  298.2 5.2 %fusion.19 = bf16[16,1,16,5120]{3,2,0,1:T(8,128)(2,1)} fusion(bf16[16,16,384]{2,1,0:T(8,128)(2,1)S(1)} %dot_general.17, bf16[384,5120]{0,1:T(8,128)(2,1)} %all-gather.5.cloned.1.call-done), kind=kOutput, calls=%fused_computation.23 | convolution fusion | flops 1007943680 | bytes 6750208 | tf_op jit(solution)/shard_map/dot_general | solution.py:162
  303.5 42.6 %reduce-scatter.2.cloned.1.call-done = bf16[2,1,16,5120]{3,2,0,1:T(8,128)(2,1)} async-done(((bf16[16,1,16,5120]{3,2,0,1:T(8,128)(2,1)}), bf16[2,1,16,5120]{3,2,0,1:T(8,128)(2,1)}) %reduce-scatter.2.cloned.1.call-update) | async-done | bytes 327696 | tf_op jit(solution)/shard_map/reduce_scatter | solution.py:168
  351.7 8.6 %collective-permute-start.1 = (bf16[4,1,32,16]{3,2,1,0:T(8,128)(2,1)S(1)}, bf16[4,1,32,16]{3,2,1,0:T(8,128)(2,1)S(1)}, u32[]{:S(2)}, u32[]{:S(2)}) collective-permute-start(bf16[4,1,32,16]{3,2,1,0:T(8,128)(2,1)S(1)} %get-tuple-element.161), channel_id=1, source_target_pairs={{0,8},{8,16},{16,24},{24,32},{32,40},{40,48},{48,56},{56,64},{64,7... | collective-permute-start | bytes 12296 | tf_op jit(solution)/shard_map/ppermute | solution.py:31
  (142 shorter events, 81.0 us)
Async XLA Ops:
  7.2 340.5 %copy-start = (bf16[5120,64]{0,1:T(8,128)(2,1)S(1)}, bf16[5120,64]{0,1:T(8,128)(2,1)}, u32[]{:S(2)}) copy-start(bf16[5120,64]{0,1:T(8,128)(2,1)} %param.23) | copy-start | bytes 1966084
  7.2 13.5 %copy-start.5 = (bf16[2,1,16,3072]{3,2,1,0:T(8,128)(2,1)S(1)}, bf16[2,1,16,3072]{3,2,1,0:T(8,128)(2,1)}, u32[]{:S(2)}) copy-start(bf16[2,1,16,3072]{3,2,1,0:T(8,128)(2,1)} %param.17) | copy-start | bytes 589828
  12.8 16.5 %all-to-all-start = ((bf16[8,2,6144]{2,1,0:T(2,128)(2,1)}), bf16[8,2,6144]{2,1,0:T(2,128)(2,1)S(1)}, u32[]{:S(2)}, u32[]{:S(2)}) async-start(bf16[8,2,6144]{2,1,0:T(2,128)(2,1)} %reshape.128), calls=%async_computation | async-start | bytes 393216 | tf_op jit(solution)/shard_map/all_to_all | solution.py:141
  29.3 12.0 %all-to-all-start.1 = ((bf16[8,2,6144]{2,1,0:T(2,128)(2,1)}), bf16[8,2,6144]{2,1,0:T(2,128)(2,1)S(1)}, u32[]{:S(2)}, u32[]{:S(2)}) async-start(bf16[8,2,6144]{2,1,0:T(2,128)(2,1)} %reshape.126), calls=%async_computation.1 | async-start | bytes 393216 | tf_op jit(solution)/shard_map/all_to_all | solution.py:142
  32.9 132.3 %all-gather.3.cloned.1.call-start = ((), (), s32[]{:S(2)}) async-start(), calls=%async_computation.4 | async-start | bytes 12976128 | tf_op jit(solution)/shard_map/all_gather | solution.py:11
  35.0 9.2 %copy-start.6 = (bf16[2,1,16,3072]{3,2,1,0:T(8,128)(2,1)S(1)}, bf16[2,1,16,3072]{3,2,1,0:T(8,128)(2,1)}, u32[]{:S(2)}) copy-start(bf16[2,1,16,3072]{3,2,1,0:T(8,128)(2,1)} %param.15) | copy-start | bytes 589828
  48.4 12.0 %all-to-all-start.2 = ((bf16[8,2,6144]{2,1,0:T(2,128)(2,1)}), bf16[8,2,6144]{2,1,0:T(2,128)(2,1)S(1)}, u32[]{:S(2)}, u32[]{:S(2)}) async-start(bf16[8,2,6144]{2,1,0:T(2,128)(2,1)} %reshape.130), calls=%async_computation.2 | async-start | bytes 393216 | tf_op jit(solution)/shard_map/all_to_all | solution.py:140
  52.0 246.1 %all-gather.5.cloned.1.call-start = ((), (), s32[]{:S(2)}) async-start(), calls=%async_computation.5 | async-start | bytes 4055040 | tf_op jit(solution)/shard_map/all_gather | solution.py:164
  52.8 293.2 %reduce-scatter.2.cloned.1.call-start = ((), (), s32[]{:S(2)}) async-start(), calls=%async_computation.6 | async-start | bytes 2949120 | tf_op jit(solution)/shard_map/reduce_scatter | solution.py:168
  178.4 24.9 %slice-start = ((s8[6291456]{0:T(1024)(128)(4,1)}), s8[2097152]{0:T(1024)(128)(4,1)S(1)}, s32[]{:S(2)}) async-start(s8[6291456]{0:T(1024)(128)(4,1)} %bitcast.112), calls=%async_computation.7 | async-start | bytes 4194304
  195.2 8.1 %slice-start.1 = ((s8[6291456]{0:T(1024)(128)(4,1)}), s8[4194304]{0:T(1024)(128)(4,1)S(1)}, s32[]{:S(2)}) async-start(s8[6291456]{0:T(1024)(128)(4,1)} %bitcast.112), calls=%async_computation.8 | async-start | bytes 8388608
  243.0 2.8 copy-start.1
  298.1 5.4 %copy-start.8 = (f32[5120]{0:T(1024)S(1)}, f32[5120]{0:T(1024)}, u32[]{:S(2)}) copy-start(f32[5120]{0:T(1024)} %param.22) | copy-start | bytes 61444
  298.1 47.9 %copy-start.4 = (bf16[2,1,16,5120]{3,2,1,0:T(8,128)(2,1)S(1)}, bf16[2,1,16,5120]{3,2,1,0:T(8,128)(2,1)}, u32[]{:S(2)}) copy-start(bf16[2,1,16,5120]{3,2,1,0:T(8,128)(2,1)} %param.18) | copy-start | bytes 983044
  298.1 47.9 %copy-start.9 = (f32[5120]{0:T(1024)S(1)}, f32[5120]{0:T(1024)}, u32[]{:S(2)}) copy-start(f32[5120]{0:T(1024)} %param.20) | copy-start | bytes 61444
  303.4 44.1 %copy-start.7 = (f32[5120]{0:T(1024)S(1)}, f32[5120]{0:T(1024)}, u32[]{:S(2)}) copy-start(f32[5120]{0:T(1024)} %param.21) | copy-start | bytes 61444
  303.4 44.3 %copy-start.12 = (f32[64]{0:T(128)S(1)}, f32[64]{0:T(128)}, u32[]{:S(2)}) copy-start(f32[64]{0:T(128)} %param.24) | copy-start | bytes 772
  303.5 62.7 %copy-start.3 = (bf16[3,3,3,16,384]{4,3,2,1,0:T(8,128)(2,1)S(1)}, bf16[3,3,3,16,384]{4,3,2,1,0:T(8,128)(2,1)}, u32[]{:S(2)}) copy-start(bf16[3,3,3,16,384]{4,3,2,1,0:T(8,128)(2,1)} %param.25) | copy-start | bytes 995332
  303.5 62.7 %copy-start.10 = (f32[384]{0:T(512)S(1)}, f32[384]{0:T(512)}, u32[]{:S(2)}) copy-start(f32[384]{0:T(512)} %param.26) | copy-start | bytes 4612
  347.2 19.2 %copy-start.2 = (bf16[2,1,16,5120]{3,2,0,1:T(8,128)(2,1)}, bf16[2,1,16,5120]{3,2,0,1:T(8,128)(2,1)S(1)}, u32[]{:S(2)}) copy-start(bf16[2,1,16,5120]{3,2,0,1:T(8,128)(2,1)S(1)} %get-tuple-element.130) | copy-start | bytes 983044
  347.3 19.2 %copy-start.11 = (f32[384]{0:T(512)S(1)}, f32[384]{0:T(512)}, u32[]{:S(2)}) copy-start(f32[384]{0:T(512)} %param.27) | copy-start | bytes 4612
  348.2 3.5 collective-permute-start
  351.7 10.6 %collective-permute-start.1 = (bf16[4,1,32,16]{3,2,1,0:T(8,128)(2,1)S(1)}, bf16[4,1,32,16]{3,2,1,0:T(8,128)(2,1)S(1)}, u32[]{:S(2)}, u32[]{:S(2)}) collective-permute-start(bf16[4,1,32,16]{3,2,1,0:T(8,128)(2,1)S(1)} %get-tuple-element.161), channel_id=1, source_target_pairs={{0,8},{8,16},{16,24},{24,32},{32,40},{40,48},{48,56},{56,64},{64,7... | collective-permute-start | bytes 12296 | tf_op jit(solution)/shard_map/ppermute | solution.py:31
  360.3 5.3 %collective-permute-start.2 = (bf16[4,1,32,16]{3,2,1,0:T(8,128)(2,1)S(1)}, bf16[4,1,32,16]{3,2,1,0:T(8,128)(2,1)S(1)}, u32[]{:S(2)}, u32[]{:S(2)}) collective-permute-start(bf16[4,1,32,16]{3,2,1,0:T(8,128)(2,1)S(1)} %get-tuple-element.162), channel_id=1, source_target_pairs={{8,0},{16,8},{24,16},{32,24},{40,32},{48,40},{56,48},{64,56},{72,6... | collective-permute-start | bytes 12296 | tf_op jit(solution)/shard_map/ppermute | solution.py:32
  (7 other events, 19.8 us)
Sparse Core Ops, SparseCore 0:
  44.4 120.7 all-gather.2
  167.4 71.8 all-gather.4
  303.6 42.4 reduce-scatter.1
where the time goes:
time: 376 us; the launch traced here: 374 us
  waiting for transfers between devices  168 us (45%)
  local copies, waits for them, and re-layouts  89.2 us (24%)
  matrix products  49 us (13%)
  starting transfers between devices  28.4 us (8%)
  other arithmetic  24.3 us (6%)
  between operations  14.2 us (4%)
    all_gather x1, waiting for transfers between devices, side_by_side(): whole, at, outs = (lax.all_gather(both, axis, axis=dim, tiled=True), 0, [])  103 us
    reduce_scatter x1, waiting for transfers between devices, on_device(): lax.psum_scatter(partial_value.astype(jnp.bfloat16), 'head', scatter_dime...  42.6 us
    reshape x2, local copies, waits for them, and re-layouts, regroup(): one_piece.reshape(frames, height // group_rows, group_rows, breadth, head...  33.6 us
    dot_general x8, matrix products, attend_block(): jnp.einsum('hqd,khd->hqk', query_heads, block_keys, preferred_element_typ...  26.7 us
    reduce_sum x8, other arithmetic, attend_block(): denominator = denominator * factor + jnp.sum(weights, -1)  20.6 us
    unnamed x38, local copies, waits for them, and re-layouts  17.4 us
    slice x3, local copies, waits for them, and re-layouts, side_by_side(): outs.append(lax.slice_in_dim(whole, at, at + a.shape[along], axis=along))  16.7 us
    dot_general x8, matrix products, attend_block(): jnp.einsum('hqk,khd->hqd', weights.astype(jnp.bfloat16), block_values, pr...  16.5 us
  transfers between devices with their start and end apart: 9, of which 7 were waited for; matrix products, arithmetic and copies ran while one was open for 38% of the time, Pallas kernels for 0%

commit v1 on v0

--- a/solution.py
+++ b/solution.py
@@ -1,18 +1,13 @@
+import functools
+
 import jax
 import jax.numpy as jnp
 from jax import lax
+from jax.experimental import pallas as pl
+from jax.experimental.pallas import tpu as pltpu
 from jax.sharding import PartitionSpec as P
 
 HEAD_DIM = 128
-
-
-def side_by_side(arrays, axis, dim, along):
-    both = jnp.concatenate(arrays, axis=along)
-    whole, at, outs = (lax.all_gather(both, axis, axis=dim, tiled=True), 0, [])
-    for a in arrays:
-        outs.append(lax.slice_in_dim(whole, at, at + a.shape[along], axis=along))
-        at += a.shape[along]
-    return tuple(outs)
 
 
 def from_behind(value, axis, steps):
@@ -76,44 +71,201 @@
     return jax.nn.silu(normed).astype(jnp.bfloat16).reshape(frames, height, breadth, -1)
 
 
-def attend_block(carried, block_keys, block_values, query_heads):
-    running, denominator, weighted = carried
-    scores = jnp.einsum("hqd,khd->hqk", query_heads, block_keys, preferred_element_type=jnp.float32)
-    scores = scores * query_heads.shape[-1] ** (-0.5)
-    newmax = jnp.maximum(running, jnp.max(scores, -1))
-    factor = jnp.exp(running - newmax)
-    weights = jnp.exp(scores - newmax[..., None])
-    denominator = denominator * factor + jnp.sum(weights, -1)
-    product = jnp.einsum(
-        "hqk,khd->hqd",
-        weights.astype(jnp.bfloat16),
-        block_values,
-        preferred_element_type=jnp.float32,
-    )
-    weighted = weighted * factor[..., None] + product
-    return (newmax, denominator, weighted)
-
-
-def fold_pieces(query_heads, carried, pieces):
-    key_piece, value_piece = pieces
-    frames, height, breadth = (key_piece.shape[0], key_piece.shape[1], key_piece.shape[2])
-    heads_here, head_width = (query_heads.shape[0], query_heads.shape[2])
-    group_rows = 4
-
-    def regroup(one_piece):
-        shaped = one_piece.reshape(
-            frames, height // group_rows, group_rows, breadth, heads_here, head_width
-        )
-        shaped = shaped.transpose(1, 0, 2, 3, 4, 5)
-        return shaped.reshape(
-            height // group_rows, frames * group_rows * breadth, heads_here, head_width
-        )
-
-    def advance(inner, blocks):
-        return (attend_block(inner, blocks[0], blocks[1], query_heads), None)
-
-    carried, _ = lax.scan(advance, carried, (regroup(key_piece), regroup(value_piece)))
-    return carried
+MESH = pl.DeviceIdType.MESH
+
+
+def attend_kernel(nx, nz, q_in, k_in, v_in, out_ref, qbuf, kbuf, vbuf, qt, acc, stat,
+                  a2a_send, a2a_recv, ring_send, ring_recv, pair_send, pair_recv):
+    x = lax.axis_index("head")
+    s = lax.axis_index("seq")
+    z, c = s // 2, lax.rem(s, 2)
+    rows, width = k_in.shape[0], kbuf.shape[3]
+    heads = width // HEAD_DIM
+    scale = HEAD_DIM ** (-0.5)
+    half = nz // 2
+
+    def seq_of(zz, cc):
+        return lax.rem(zz + 2 * nz, nz) * 2 + cc
+
+    barrier = pltpu.get_barrier_semaphore()
+    for d in range(1, nx):
+        pl.semaphore_signal(barrier, inc=1, device_id={"head": lax.rem(x + d, nx)}, device_id_type=MESH)
+    for other in (seq_of(z + 1, c), seq_of(z - 1, c), seq_of(z, 1 - c)):
+        pl.semaphore_signal(barrier, inc=1, device_id={"seq": other}, device_id_type=MESH)
+    pl.semaphore_wait(barrier, nx + 2)
+
+    ins = (k_in, v_in, q_in)
+    mine = (kbuf.at[c, z], vbuf.at[c, z], qbuf)
+    own_rows = pl.ds(pl.multiple_of(x * rows, rows), rows)
+    own_cols = pl.ds(pl.multiple_of(x * width, width), width)
+    for i in range(3):
+        for d in range(1, nx):
+            peer = lax.rem(x + (d + 1) // 2 if d % 2 else x + nx - d // 2, nx)
+            cols = pl.ds(pl.multiple_of(peer * width, width), width)
+            pltpu.make_async_remote_copy(
+                src_ref=ins[i].at[:, cols], dst_ref=mine[i].at[own_rows, :],
+                send_sem=a2a_send.at[i], recv_sem=a2a_recv.at[i],
+                device_id={"head": peer}, device_id_type=MESH).start()
+    for i in range(3):
+        mine[i][own_rows, :] = ins[i][:, own_cols]
+
+    def all_but_one(i):
+        part = mine[i].at[pl.ds(0, rows * (nx - 1)), :]
+        return pltpu.make_async_remote_copy(
+            src_ref=part, dst_ref=part, send_sem=a2a_send.at[i], recv_sem=a2a_recv.at[i],
+            device_id={"head": lax.rem(x + 1, nx)}, device_id_type=MESH)
+
+    bufs = (kbuf, vbuf)
+
+    def hop(kv, direction, step):
+        slot = bufs[kv].at[c, lax.rem(z - direction * (step - 1) + nz, nz)]
+        flow = 2 * kv + (1 if direction > 0 else 0)
+        return pltpu.make_async_remote_copy(
+            src_ref=slot, dst_ref=slot, send_sem=ring_send.at[flow, step], recv_sem=ring_recv.at[flow, step],
+            device_id={"seq": seq_of(z + direction, c)}, device_id_type=MESH)
+
+    def landed(kv, direction, step):
+        slot = bufs[kv].at[c, lax.rem(z - direction * step + nz, nz)]
+        flow = 2 * kv + (1 if direction > 0 else 0)
+        return pltpu.make_async_remote_copy(
+            src_ref=slot, dst_ref=slot, send_sem=ring_send.at[flow, step], recv_sem=ring_recv.at[flow, step],
+            device_id={"seq": seq_of(z + direction, c)}, device_id_type=MESH)
+
+    def share(kv, zz):
+        slot = bufs[kv].at[c, zz]
+        return pltpu.make_async_remote_copy(
+            src_ref=slot, dst_ref=slot, send_sem=pair_send.at[kv, zz], recv_sem=pair_recv.at[kv, zz],
+            device_id={"seq": seq_of(z, 1 - c)}, device_id_type=MESH)
+
+    def shared(kv, zz):
+        slot = bufs[kv].at[1 - c, zz]
+        return pltpu.make_async_remote_copy(
+            src_ref=slot, dst_ref=slot, send_sem=pair_send.at[kv, zz], recv_sem=pair_recv.at[kv, zz],
+            device_id={"seq": seq_of(z, 1 - c)}, device_id_type=MESH)
+
+    for kv in range(2):
+        all_but_one(kv).wait_recv()
+        for direction in (1, -1):
+            hop(kv, direction, 1).start()
+        share(kv, z).start()
+    all_but_one(2).wait_recv()
+
+    for j in range(heads):
+        qt[j] = qbuf[:, j * HEAD_DIM:(j + 1) * HEAD_DIM].astype(jnp.float32).T.astype(jnp.bfloat16)
+    acc[...] = jnp.zeros_like(acc)
+    stat[:, 0] = jnp.full(stat[:, 0].shape, -1e30, jnp.float32)
+    stat[:, 1] = jnp.zeros_like(stat[:, 1])
+
+    def attend(lane, zz):
+        for j in range(heads):
+            cols = pl.ds(j * HEAD_DIM, HEAD_DIM)
+            scores = lax.dot_general(kbuf[lane, zz, :, cols], qt[j], (((1,), (0,)), ((), ())),
+                                     preferred_element_type=jnp.float32)
+            before = stat[j, 0]
+            peak = jnp.maximum(before, jnp.max(scores, 0, keepdims=True))
+            factor = jnp.exp((before - peak) * scale)
+            weights = jnp.exp((scores - peak) * scale)
+            stat[j, 1] = stat[j, 1] * factor + jnp.sum(weights, 0, keepdims=True)
+            stat[j, 0] = peak
+            acc[j] = acc[j] * factor + lax.dot_general(
+                vbuf[lane, zz, :, cols], weights.astype(jnp.bfloat16), (((0,), (0,)), ((), ())),
+                preferred_element_type=jnp.float32)
+
+    def last_hop(kv, direction):
+        return half if (kv == 0) == (direction > 0) else half - 1
+
+    attend(c, z)
+    for kv in range(2):
+        shared(kv, z).wait_recv()
+    attend(1 - c, z)
+
+    def step(h, carry):
+        for kv in range(2):
+            for direction in (1, -1):
+                landed(kv, direction, h).wait_recv()
+
+                @pl.when(h < last_hop(kv, direction))
+                def _():
+                    hop(kv, direction, h + 1).start()
+
+                share(kv, lax.rem(z - direction * h + nz, nz)).start()
+
+        def block(i, carry):
+            zz = lax.rem(z - (1 - 2 * i) * h + nz, nz)
+            attend(c, zz)
+            for kv in range(2):
+                shared(kv, zz).wait_recv()
+            attend(1 - c, zz)
+            return carry
+
+        lax.fori_loop(0, 2, block, 0)
+        return carry
+
+    lax.fori_loop(1, half, step, 0)
+    far = lax.rem(z + half, nz)
+    for kv in range(2):
+        landed(kv, 1 if kv == 0 else -1, half).wait_recv()
+        share(kv, far).start()
+    attend(c, far)
+    for kv in range(2):
+        shared(kv, far).wait_recv()
+    attend(1 - c, far)
+
+    for j in range(heads):
+        whole = acc[j] / stat[j, 1]
+        out_ref[:, j * HEAD_DIM:(j + 1) * HEAD_DIM] = whole.T.astype(out_ref.dtype)
+
+    for i in range(3):
+        all_but_one(i).wait_send()
+
+    def drain(h, carry):
+        for kv in range(2):
+            for direction in (1, -1):
+                @pl.when(h <= last_hop(kv, direction))
+                def _():
+                    hop(kv, direction, h).wait_send()
+        return carry
+
+    lax.fori_loop(1, half + 1, drain, 0)
+
+    def drain_pair(zz, carry):
+        for kv in range(2):
+            share(kv, zz).wait_send()
+        return carry
+
+    lax.fori_loop(0, nz, drain_pair, 0)
+
+
+def attention(queries, attn_keys, attn_values):
+    nx, nz = lax.axis_size("head"), lax.axis_size("seq") // 2
+    frames, height, breadth, features = queries.shape
+    rows, width = frames * height * breadth, features // nx
+    heads = width // HEAD_DIM
+    count = rows * nx
+    flat = [a.reshape(rows, features) for a in (queries, attn_keys, attn_values)]
+    kept = pl.BlockSpec(memory_space=pltpu.VMEM)
+    dma = pltpu.SemaphoreType.DMA
+    return pl.pallas_call(
+        functools.partial(attend_kernel, nx, nz),
+        out_shape=jax.ShapeDtypeStruct((count, width), jnp.bfloat16),
+        in_specs=[kept] * 3,
+        out_specs=kept,
+        scratch_shapes=[
+            pltpu.VMEM((count, width), jnp.bfloat16),
+            pltpu.VMEM((2, nz, count, width), jnp.bfloat16),
+            pltpu.VMEM((2, nz, count, width), jnp.bfloat16),
+            pltpu.VMEM((heads, HEAD_DIM, count), jnp.bfloat16),
+            pltpu.VMEM((heads, HEAD_DIM, count), jnp.float32),
+            pltpu.VMEM((heads, 2, 1, count), jnp.float32),
+            dma((3,)), dma((3,)),
+            dma((4, nz // 2 + 1)), dma((4, nz // 2 + 1)),
+            dma((2, nz)), dma((2, nz)),
+        ],
+        compiler_params=pltpu.CompilerParams(
+            collective_id=0, has_side_effects=True, vmem_limit_bytes=40 * 2**20),
+        cost_estimate=pl.CostEstimate(flops=4 * count * count * 2 * nz * width, bytes_accessed=2**21, transcendentals=0),
+        name="attention_ring",
+    )(*flat)
 
 
 def on_device(
@@ -131,34 +283,9 @@
     conv_bias,
     norm_gain,
 ):
-    head_count = lax.axis_size("head")
-    frames_dev = queries.shape[0]
-    group_width = queries.shape[3] // head_count
-    head_width = HEAD_DIM
-    heads_here = group_width // head_width
-    local_queries, local_keys, local_values = (
-        lax.all_to_all(queries, "head", split_axis=3, concat_axis=0, tiled=True),
-        lax.all_to_all(attn_keys, "head", split_axis=3, concat_axis=0, tiled=True),
-        lax.all_to_all(attn_values, "head", split_axis=3, concat_axis=0, tiled=True),
-    )
-    frames_all, height, breadth = (
-        local_queries.shape[0],
-        local_queries.shape[1],
-        local_queries.shape[2],
-    )
-    count = frames_all * height * breadth
-    query_heads = local_queries.reshape(count, heads_here, head_width).transpose(1, 0, 2)
-    initial = (
-        jnp.full((heads_here, count), -1e30, jnp.float32),
-        jnp.zeros((heads_here, count), jnp.float32),
-        jnp.zeros((heads_here, count, head_width), jnp.float32),
-    )
-    carried = fold_pieces(
-        query_heads, initial, side_by_side((local_keys, local_values), "seq", 1, 0)
-    )
-    running, denominator, weighted = carried
-    attended = (weighted / denominator[..., None]).astype(jnp.bfloat16)
-    attended = attended.transpose(1, 0, 2).reshape(count, group_width)
+    frames_dev, height, breadth = queries.shape[:3]
+    frames_all = frames_dev * lax.axis_size("head")
+    attended = attention(queries, attn_keys, attn_values)
     partial_value = jnp.dot(
         attended,
         lax.all_gather(out_weight, "seq", axis=1, tiled=True),

time: 376 us -> 226 us (0.60)
  Pallas kernels: 0 us -> 143 us
  waiting for transfers between devices: 168 us -> 43.5 us
  local copies, waits for them, and re-layouts: 89.2 us -> 3.42 us
  matrix products: 49 us -> 5.85 us
  other arithmetic: 24.3 us -> 2.54 us
  starting transfers between devices: 28.4 us -> 13.2 us
    pallas_call x0 -> x1, Pallas kernels: none -> 143 us  [attention(): pl.pallas_call(functools.partial(attend_kernel, nx, nz), out_shape=jax.Sh...]
    all_gather x1 -> x0, waiting for transfers between devices: 103 us -> none  [side_by_side(): whole, at, outs = (lax.all_gather(both, axis, axis=dim, tiled=True), 0, [])]
    dot_general x16 -> x0, matrix products: 43.2 us -> none  [the longest x8 26.7 us: attend_block(): jnp.einsum('hqd,khd->hqk', query_heads, block_keys, preferred_element_typ...]
    reshape x3 -> x0, local copies, waits for them, and re-layouts: 33.6 us -> none  [the longest x2 33.6 us: regroup(): one_piece.reshape(frames, height // group_rows, group_rows, breadth, head...]
    reduce_sum x8 -> x0, other arithmetic: 20.6 us -> none  [attend_block(): denominator = denominator * factor + jnp.sum(weights, -1)]
    all_to_all x3 -> x0, waiting for transfers between devices: 18 us -> none  [the longest x1 7.29 us: on_device(): lax.all_to_all(queries, 'head', split_axis=3, concat_axis=0, tiled=True)]
    slice x3 -> x0, local copies, waits for them, and re-layouts: 16.7 us -> none  [side_by_side(): outs.append(lax.slice_in_dim(whole, at, at + a.shape[along], axis=along))]
    transpose x3 -> x0, local copies, waits for them, and re-layouts: 16.1 us -> none  [the longest x2 15.9 us: regroup(): shaped = shaped.transpose(1, 0, 2, 3, 4, 5)]
  transfers between devices with their start and end apart: 9 -> 5, of which waited for: 7 -> 3; matrix products, arithmetic and copies ran while one was open for 38% -> 0% of each run, Pallas kernels for 0% -> 63%
where the time goes in v1:
time: 226 us
  Pallas kernels  143 us (63%)
  waiting for transfers between devices  43.5 us (19%)
  between operations  14.3 us (6%)
  starting transfers between devices  13.2 us (6%)
  matrix products  5.85 us (3%)
  local copies, waits for them, and re-layouts  3.42 us (2%)
  other arithmetic  2.54 us (1%)
    pallas_call x1, Pallas kernels, attention(): pl.pallas_call(functools.partial(attend_kernel, nx, nz), out_shape=jax.Sh...  143 us
    reduce_scatter x1, waiting for transfers between devices, on_device(): lax.psum_scatter(partial_value.astype(jnp.bfloat16), 'head', scatter_dime...  38.4 us
    ppermute x1, starting transfers between devices, padded_2(): before = lax.ppermute(last, axis, up)  8.43 us
    dot_general x1, matrix products, on_device(): jnp.dot(attended, lax.all_gather(out_weight, 'seq', axis=1, tiled=True),...  5.23 us
  transfers between devices with their start and end apart: 5, of which 3 were waited for; matrix products, arithmetic and copies ran while one was open for 0% of the time, Pallas kernels for 63%

profile of v1, /device:TPU:65, one launch (start us, length us, event | category | flops | bytes accessed | tf_op | source)
XLA Modules:
  0.0 226.2 jit_solution(14802032481148267061)
XLA Ops:
  7.2 0.1 all-gather.2.cloned.1.call-start
  7.3 0.7 all-gather.2.cloned.1.call-update
  8.0 0.1 reduce-scatter.2.cloned.1.call-start
  8.1 0.9 copy-done.1
  9.0 0.9 copy-done.2
  9.9 0.9 copy-done.3
  10.8 143.4 %attention_ring.1 = bf16[256,384]{1,0:T(8,128)(2,1)S(1)} custom-call(bf16[32,3072]{1,0:T(8,128)(2,1)S(1)} %bitcast.46, bf16[32,3072]{1,0:T(8,128)(2,1)S(1)} %bitcast.47, bf16[32,3072]{1,0:T(8,128)(2,1)S(1)} %bitcast.48), custom_call_target="tpu_custom_call" | custom-call | flops 3221225472 | bytes 2097152 | tf_op jit(solution)/shard_map/attention_ring/pallas_call | solution.py:248
  154.3 5.2 %convolution_convert_fusion = bf16[256,5120]{1,0:T(8,128)(2,1)} fusion(bf16[256,384]{1,0:T(8,128)(2,1)S(1)} %attention_ring.1, bf16[384,5120]{0,1:T(8,128)(2,1)} %all-gather.2.cloned.1.call-done), kind=kOutput, calls=%fused_computation | convolution fusion | flops 1007943680 | bytes 6750208 | tf_op jit(solution)/shard_map/dot_general | solution.py:289
  159.7 38.4 %reduce-scatter.2.cloned.1.call-done = bf16[2,1,16,5120]{3,2,1,0:T(8,128)(2,1)} async-done(((bf16[16,1,16,5120]{3,2,1,0:T(8,128)(2,1)}), bf16[2,1,16,5120]{3,2,1,0:T(8,128)(2,1)}) %reduce-scatter.2.cloned.1.call-update) | async-done | bytes 327696 | tf_op jit(solution)/shard_map/reduce_scatter | solution.py:295
  198.1 1.2 convert_reduce_fusion
  199.3 0.2 fusion.3
  199.5 0.2 fusion.6
  199.7 0.3 fusion
  200.1 0.1 reshape.117
  200.2 2.7 %collective-permute-start = (bf16[2,2,32,16]{3,2,1,0:T(8,128)(2,1)S(1)}, bf16[2,2,32,16]{3,2,1,0:T(8,128)(2,1)S(1)}, u32[]{:S(2)}, u32[]{:S(2)}) collective-permute-start(bf16[2,2,32,16]{3,2,1,0:T(8,128)(2,1)S(1)} %bitcast.51), channel_id=1, source_target_pairs={{0,1},{1,2},{2,3},{3,4},{4,5},{5,6},{6,7},{8,9},{9,10},{10,11},{11... | collective-permute-start | bytes 12296 | tf_op jit(solution)/shard_map/ppermute | solution.py:16
  202.9 1.0 collective-permute-done
  203.9 8.4 %collective-permute-start.1 = (bf16[4,1,32,16]{3,2,1,0:T(8,128)(2,1)S(1)}, bf16[4,1,32,16]{3,2,1,0:T(8,128)(2,1)S(1)}, u32[]{:S(2)}, u32[]{:S(2)}) collective-permute-start(bf16[4,1,32,16]{3,2,1,0:T(8,128)(2,1)S(1)} %get-tuple-element.30), channel_id=1, source_target_pairs={{0,8},{8,16},{16,24},{24,32},{32,40},{40,48},{48,56},{56,64},{64,7... | collective-permute-start | bytes 12296 | tf_op jit(solution)/shard_map/ppermute | solution.py:26
  212.4 2.0 collective-permute-start.2
  214.3 3.3 %collective-permute-done.2 = bf16[4,1,32,16]{3,2,1,0:T(8,128)(2,1)S(1)} collective-permute-done((bf16[4,1,32,16]{3,2,1,0:T(8,128)(2,1)S(1)}, bf16[4,1,32,16]{3,2,1,0:T(8,128)(2,1)S(1)}, u32[]{:S(2)}, u32[]{:S(2)}) %collective-permute-start.2) | collective-permute-done | bytes 4128 | tf_op jit(solution)/shard_map/ppermute | solution.py:27
  217.6 0.1 select_maximum_fusion
  217.7 0.1 fusion.13
  217.9 0.3 concatenate.105
  218.2 0.3 multiply_reduce_fusion
  218.6 0.8 multiply_convert_fusion
  (35 shorter events, 0.3 us)
Async XLA Ops:
  7.2 192.5 %copy-start = (bf16[5120,64]{0,1:T(8,128)(2,1)S(1)}, bf16[5120,64]{0,1:T(8,128)(2,1)}, u32[]{:S(2)}) copy-start(bf16[5120,64]{0,1:T(8,128)(2,1)} %param.21) | copy-start | bytes 1966084
  7.2 147.1 %all-gather.2.cloned.1.call-start = ((), (), s32[]{:S(2)}) async-start(), calls=%async_computation.1 | async-start | bytes 4055040 | tf_op jit(solution)/shard_map/all_gather | solution.py:291
  8.0 190.1 %reduce-scatter.2.cloned.1.call-start = ((), (), s32[]{:S(2)}) async-start(), calls=%async_computation.2 | async-start | bytes 2949120 | tf_op jit(solution)/shard_map/reduce_scatter | solution.py:295
  8.1 0.9 copy-start.1
  9.0 0.9 copy-start.2
  9.9 0.9 copy-start.3
  154.2 5.4 %copy-start.8 = (f32[5120]{0:T(1024)S(1)}, f32[5120]{0:T(1024)}, u32[]{:S(2)}) copy-start(f32[5120]{0:T(1024)} %param.20) | copy-start | bytes 61444
  154.2 43.8 %copy-start.6 = (bf16[2,1,16,5120]{3,2,1,0:T(8,128)(2,1)S(1)}, bf16[2,1,16,5120]{3,2,1,0:T(8,128)(2,1)}, u32[]{:S(2)}) copy-start(bf16[2,1,16,5120]{3,2,1,0:T(8,128)(2,1)} %param.16) | copy-start | bytes 983044
  154.2 43.8 %copy-start.9 = (f32[5120]{0:T(1024)S(1)}, f32[5120]{0:T(1024)}, u32[]{:S(2)}) copy-start(f32[5120]{0:T(1024)} %param.18) | copy-start | bytes 61444
  154.3 45.3 %copy-start.7 = (f32[5120]{0:T(1024)S(1)}, f32[5120]{0:T(1024)}, u32[]{:S(2)}) copy-start(f32[5120]{0:T(1024)} %param.19) | copy-start | bytes 61444
  159.5 40.2 %copy-start.12 = (f32[64]{0:T(128)S(1)}, f32[64]{0:T(128)}, u32[]{:S(2)}) copy-start(f32[64]{0:T(128)} %param.22) | copy-start | bytes 772
  159.6 58.6 %copy-start.5 = (bf16[3,3,3,16,384]{4,3,2,1,0:T(8,128)(2,1)S(1)}, bf16[3,3,3,16,384]{4,3,2,1,0:T(8,128)(2,1)}, u32[]{:S(2)}) copy-start(bf16[3,3,3,16,384]{4,3,2,1,0:T(8,128)(2,1)} %param.23) | copy-start | bytes 995332
  159.6 58.6 %copy-start.10 = (f32[384]{0:T(512)S(1)}, f32[384]{0:T(512)}, u32[]{:S(2)}) copy-start(f32[384]{0:T(512)} %param.24) | copy-start | bytes 4612
  159.6 58.9 %copy-start.11 = (f32[384]{0:T(512)S(1)}, f32[384]{0:T(512)}, u32[]{:S(2)}) copy-start(f32[384]{0:T(512)} %param.25) | copy-start | bytes 4612
  199.2 20.1 %copy-start.4 = (bf16[2,1,16,5120]{3,2,1,0:T(8,128)(2,1)}, bf16[2,1,16,5120]{3,2,1,0:T(8,128)(2,1)S(1)}, u32[]{:S(2)}) copy-start(bf16[2,1,16,5120]{3,2,1,0:T(8,128)(2,1)S(1)} %get-tuple-element.3) | copy-start | bytes 983044
  200.2 3.7 %collective-permute-start = (bf16[2,2,32,16]{3,2,1,0:T(8,128)(2,1)S(1)}, bf16[2,2,32,16]{3,2,1,0:T(8,128)(2,1)S(1)}, u32[]{:S(2)}, u32[]{:S(2)}) collective-permute-start(bf16[2,2,32,16]{3,2,1,0:T(8,128)(2,1)S(1)} %bitcast.51), channel_id=1, source_target_pairs={{0,1},{1,2},{2,3},{3,4},{4,5},{5,6},{6,7},{8,9},{9,10},{10,11},{11... | collective-permute-start | bytes 12296 | tf_op jit(solution)/shard_map/ppermute | solution.py:16
  203.9 10.4 %collective-permute-start.1 = (bf16[4,1,32,16]{3,2,1,0:T(8,128)(2,1)S(1)}, bf16[4,1,32,16]{3,2,1,0:T(8,128)(2,1)S(1)}, u32[]{:S(2)}, u32[]{:S(2)}) collective-permute-start(bf16[4,1,32,16]{3,2,1,0:T(8,128)(2,1)S(1)} %get-tuple-element.30), channel_id=1, source_target_pairs={{0,8},{8,16},{16,24},{24,32},{32,40},{40,48},{48,56},{56,64},{64,7... | collective-permute-start | bytes 12296 | tf_op jit(solution)/shard_map/ppermute | solution.py:26
  212.4 5.3 %collective-permute-start.2 = (bf16[4,1,32,16]{3,2,1,0:T(8,128)(2,1)S(1)}, bf16[4,1,32,16]{3,2,1,0:T(8,128)(2,1)S(1)}, u32[]{:S(2)}, u32[]{:S(2)}) collective-permute-start(bf16[4,1,32,16]{3,2,1,0:T(8,128)(2,1)S(1)} %get-tuple-element.31), channel_id=1, source_target_pairs={{8,0},{16,8},{24,16},{32,24},{40,32},{48,40},{56,48},{64,56},{72,6... | collective-permute-start | bytes 12296 | tf_op jit(solution)/shard_map/ppermute | solution.py:27
Sparse Core Ops, SparseCore 0:
  10.2 115.4 all-gather.1
  159.7 38.2 reduce-scatter.1

commit v2 on v1

v2 whole, which is shorter than its diff:
```python
import functools

import jax
import jax.numpy as jnp
from jax import lax
from jax.experimental import pallas as pl
from jax.experimental.pallas import tpu as pltpu
from jax.sharding import PartitionSpec as P

HEAD_DIM = 128
MESH = pl.DeviceIdType.MESH
SUBS = 2


def convolve(padded, frames, conv_weight, conv_bias, norm_gain):
    height = padded.shape[1] - 2
    breadth = padded.shape[2] - 2
    stacked = jnp.concatenate(
        [
            padded[
                time_off : time_off + frames,
                row_off : row_off + height,
                col_off : col_off + breadth,
            ]
            for time_off in range(3)
            for row_off in range(3)
            for col_off in range(3)
        ],
        -1,
    )
    kernel = conv_weight.reshape(-1, conv_weight.shape[-1])
    linear = (
        jnp.dot(stacked.reshape(-1, stacked.shape[-1]), kernel, preferred_element_type=jnp.float32)
        + conv_bias
    )
    normed = linear * lax.rsqrt(jnp.mean(linear * linear, -1, keepdims=True) + 1e-06) * norm_gain
    return jax.nn.silu(normed).astype(jnp.bfloat16).reshape(frames, height, breadth, -1)


def block_kernel(nx, nz, q_in, k_in, v_in, w_in, res_in, gate_in, shift_in, scale_in, hw_in, hb_in,
                 hidden_ref, lat_ref,
                 qbuf, kbuf, vbuf, wbuf, qt, acc, stat, part, sums_out, sums_in, tokens, owned, lat,
                 res, gate, shift, gain, hw, hb,
                 local_sem, a2a_send, a2a_recv, ring_send, ring_recv, pair_send, pair_recv,
                 w_send, w_recv, wpair_send, wpair_recv, rs_send, rs_recv, halo_send, halo_recv, out_sem):
    x = lax.axis_index("head")
    s = lax.axis_index("seq")
    z, c = s // 2, lax.rem(s, 2)
    nseq = 2 * nz
    rows, width = k_in.shape[0], kbuf.shape[3]
    heads = width // HEAD_DIM
    scale = HEAD_DIM ** (-0.5)
    half = nz // 2
    features = part.shape[1]

    def seq_of(zz, cc):
        return lax.rem(zz + 2 * nz, nz) * 2 + cc

    def remote(src, dst, send, recv, **where):
        return pltpu.make_async_remote_copy(
            src_ref=src, dst_ref=dst, send_sem=send, recv_sem=recv, device_id=where, device_id_type=MESH)

    own_rows = pl.ds(pl.multiple_of(x * rows, rows), rows)
    own_cols = pl.ds(pl.multiple_of(x * width, width), width)
    mine = (kbuf.at[c, z], vbuf.at[c, z], qbuf)
    ins = (k_in, v_in, q_in)
    loads = [pltpu.make_async_copy(ins[i].at[:, own_cols], mine[i].at[own_rows, :], local_sem.at[i]) for i in range(3)]
    loads.append(pltpu.make_async_copy(w_in, wbuf.at[z, c], local_sem.at[3]))
    late = ((res_in, res), (gate_in, gate), (shift_in, shift), (scale_in, gain), (hw_in, hw), (hb_in, hb))
    loads += [pltpu.make_async_copy(a, b, local_sem.at[4 + i]) for i, (a, b) in enumerate(late)]
    for load in loads:
        load.start()

    def away(value, by, size):
        return lax.rem(value + by + size, size)

    lat[...] = jnp.zeros_like(lat)
    barrier = pltpu.get_barrier_semaphore()
    for d in range(1, nx):
        pl.semaphore_signal(barrier, inc=1, device_id={"head": away(x, d, nx)}, device_id_type=MESH)
    for other in (seq_of(z + 1, c), seq_of(z - 1, c), seq_of(z, 1 - c), away(s, 2 * c - 1, nseq)):
        pl.semaphore_signal(barrier, inc=1, device_id={"seq": other}, device_id_type=MESH)
    for dx in (1, -1):
        for ds in (1, -1):
            pl.semaphore_signal(barrier, inc=1, device_id={"head": away(x, dx, nx), "seq": away(s, ds, nseq)},
                                device_id_type=MESH)
    pl.semaphore_wait(barrier, nx + 7)

    for i in range(3):
        for d in range(1, nx):
            peer = lax.rem(x + (d + 1) // 2 if d % 2 else x + nx - d // 2, nx)
            cols = pl.ds(pl.multiple_of(peer * width, width), width)
            remote(ins[i].at[:, cols], mine[i].at[own_rows, :], a2a_send.at[i], a2a_recv.at[i], head=peer).start()

    def all_but_one(i):
        piece = mine[i].at[pl.ds(0, rows * (nx - 1)), :]
        return remote(piece, piece, a2a_send.at[i], a2a_recv.at[i], head=away(x, 1, nx))

    bufs = (kbuf, vbuf)

    def hop(kv, direction, step, back):
        slot = bufs[kv].at[c, lax.rem(z - direction * back + 2 * nz, nz)]
        flow = 2 * kv + (1 if direction > 0 else 0)
        return remote(slot, slot, ring_send.at[flow, step], ring_recv.at[flow, step], seq=seq_of(z + direction, c))

    def w_hop(direction, step, back):
        slot = wbuf.at[lax.rem(z - direction * back + 2 * nz, nz), c]
        flow = 1 if direction > 0 else 0
        return remote(slot, slot, w_send.at[flow, step], w_recv.at[flow, step], seq=seq_of(z + direction, c))

    def share(kv, zz, cc):
        slot = bufs[kv].at[cc, zz]
        return remote(slot, slot, pair_send.at[kv, zz], pair_recv.at[kv, zz], seq=seq_of(z, 1 - c))

    def w_share(zz, cc):
        slot = wbuf.at[zz, cc]
        return remote(slot, slot, wpair_send.at[zz], wpair_recv.at[zz], seq=seq_of(z, 1 - c))

    loads[3].wait()
    for direction in (1, -1):
        w_hop(direction, 1, 0).start()
    w_share(z, c).start()
    for kv in range(2):
        loads[kv].wait()
        all_but_one(kv).wait_recv()
        for direction in (1, -1):
            hop(kv, direction, 1, 0).start()
        share(kv, z, c).start()
    loads[2].wait()
    all_but_one(2).wait_recv()

    for j in range(heads):
        qt[j] = qbuf[:, j * HEAD_DIM:(j + 1) * HEAD_DIM].astype(jnp.float32).T.astype(jnp.bfloat16)
    acc[...] = jnp.zeros_like(acc)
    stat[:, 0] = jnp.full(stat[:, 0].shape, -1e30, jnp.float32)
    stat[:, 1] = jnp.zeros_like(stat[:, 1])

    def attend(lane, zz):
        for j in range(heads):
            cols = pl.ds(j * HEAD_DIM, HEAD_DIM)
            scores = lax.dot_general(kbuf[lane, zz, :, cols], qt[j], (((1,), (0,)), ((), ())),
                                     preferred_element_type=jnp.float32)
            before = stat[j, 0]
            peak = jnp.maximum(before, jnp.max(scores, 0, keepdims=True))
            factor = jnp.exp((before - peak) * scale)
            weights = jnp.exp((scores - peak) * scale)
            stat[j, 1] = stat[j, 1] * factor + jnp.sum(weights, 0, keepdims=True)
            stat[j, 0] = peak
            acc[j] = acc[j] * factor + lax.dot_general(
                vbuf[lane, zz, :, cols], weights.astype(jnp.bfloat16), (((0,), (0,)), ((), ())),
                preferred_element_type=jnp.float32)

    def last_hop(kv, direction):
        return half if (kv == 0) == (direction > 0) else half - 1

    def w_last(direction):
        return half if direction > 0 else half - 1

    def both_lanes(zz):
        attend(c, zz)
        for kv in range(2):
            share(kv, zz, 1 - c).wait_recv()
        attend(1 - c, zz)

    both_lanes(z)

    def step(h, carry):
        for kv in range(2):
            for direction in (1, -1):
                hop(kv, direction, h, h).wait_recv()

                @pl.when(h < last_hop(kv, direction))
                def _():
                    hop(kv, direction, h + 1, h).start()

                share(kv, lax.rem(z - direction * h + nz, nz), c).start()
        for direction in (1, -1):
            w_hop(direction, h, h).wait_recv()

            @pl.when(h < w_last(direction))
            def _():
                w_hop(direction, h + 1, h).start()

            w_share(lax.rem(z - direction * h + nz, nz), c).start()

        def block(i, carry):
            both_lanes(lax.rem(z - (1 - 2 * i) * h + nz, nz))
            return carry

        lax.fori_loop(0, 2, block, 0)
        return carry

    lax.fori_loop(1, half, step, 0)
    far = lax.rem(z + half, nz)
    for kv in range(2):
        hop(kv, 1 if kv == 0 else -1, half, half).wait_recv()
        share(kv, far, c).start()
    w_hop(1, half, half).wait_recv()
    w_share(far, c).start()
    both_lanes(far)

    for j in range(heads):
        tokens[:, j * HEAD_DIM:(j + 1) * HEAD_DIM] = (acc[j] / stat[j, 1]).T.astype(jnp.bfloat16)

    def w_land(zz, carry):
        w_share(zz, 1 - c).wait_recv()
        return carry

    lax.fori_loop(0, nz, w_land, 0)

    w_rows = w_in.shape[0]
    tile = 4 * w_rows

    def project(i, carry):
        columns = wbuf[pl.ds(2 * i, 2)].reshape(tile, width)
        part[:, pl.ds(pl.multiple_of(i * tile, tile), tile)] = lax.dot_general(
            tokens[...], columns, (((1,), (1,)), ((), ())), preferred_element_type=jnp.float32)
        return carry

    lax.fori_loop(0, nz // 2, project, 0)
    block = features // (2 * SUBS)

    def term(flow, direction, t):
        owner = lax.rem(x - direction * t + 2 * nx, nx)
        return part[pl.ds(pl.multiple_of(owner * rows, rows), rows), flow * block:(flow + 1) * block]

    def rs(flow, direction, t):
        return remote(sums_out.at[flow, t], sums_in.at[flow, t], rs_send.at[flow, t], rs_recv.at[flow, t],
                      head=away(x, direction, nx))

    flows = [(f, 1 if f % 2 else -1) for f in range(2 * SUBS)]
    for f, direction in flows:
        sums_out[f, 1] = term(f, direction, 1).astype(jnp.bfloat16)
    for f, direction in flows:
        rs(f, direction, 1).start()

    def rs_step(t, carry):
        for f, direction in flows:
            rs(f, direction, t - 1).wait_recv()
            sums_out[f, t] = (sums_in[f, t - 1].astype(jnp.float32) + term(f, direction, t)).astype(jnp.bfloat16)
            rs(f, direction, t).start()
        return carry

    lax.fori_loop(2, nx, rs_step, 0)
    for load in loads[4:]:
        load.wait()
    for f, direction in flows:
        rs(f, direction, nx - 1).wait_recv()
        cols = slice(f * block, (f + 1) * block)
        total = sums_in[f, nx - 1].astype(jnp.float32) + term(f, direction, nx)
        owned[:, cols] = (res[:, cols].astype(jnp.float32) + gate[:, cols] * total).astype(jnp.bfloat16)

    out = pltpu.make_async_copy(owned, hidden_ref, out_sem.at[0])
    out.start()
    values = owned[...].astype(jnp.float32)
    center = values - jnp.mean(values, -1, keepdims=True)
    spread = jnp.mean(center * center, -1, keepdims=True)
    normed = (center * lax.rsqrt(spread + 1e-06) * (1.0 + gain[...]) + shift[...]).astype(jnp.bfloat16)
    latent = jnp.dot(normed, hw[...], preferred_element_type=jnp.float32) + hb[...]
    cells = latent.shape[1]
    lat[1, 1, :, 0:cells] = latent.astype(jnp.bfloat16)

    sends = []
    for i, (dx, ds) in enumerate(((0, 1), (0, -1), (1, 0), (1, 1), (1, -1))):
        def copy(i=i, dx=dx, ds=ds):
            return remote(lat.at[1, 1], lat.at[1 - dx, 1 - ds], halo_send.at[i], halo_recv.at[i],
                          head=away(x, dx, nx), seq=away(s, ds, nseq))
        goes, comes = s >= 0, s >= 0
        if ds:
            goes = goes & (s + ds >= 0) & (s + ds < nseq)
            comes = comes & (s - ds >= 0) & (s - ds < nseq)
        if dx:
            goes = goes & (x + 1 < nx)
            comes = comes & (x > 0)
        sends.append((copy, goes, comes))
    for copy, goes, comes in sends:
        @pl.when(goes)
        def _():
            copy().start()

    for i in range(3):
        all_but_one(i).wait_send()

    def drain(h, carry):
        for kv in range(2):
            for direction in (1, -1):
                @pl.when(h <= last_hop(kv, direction))
                def _():
                    hop(kv, direction, h, h - 1).wait_send()
        for direction in (1, -1):
            @pl.when(h <= w_last(direction))
            def _():
                w_hop(direction, h, h - 1).wait_send()
        return carry

    lax.fori_loop(1, half + 1, drain, 0)

    def drain_pair(zz, carry):
        for kv in range(2):
            share(kv, zz, c).wait_send()
        w_share(zz, c).wait_send()
        return carry

    lax.fori_loop(0, nz, drain_pair, 0)

    def drain_rs(t, carry):
        for f, direction in flows:
            rs(f, direction, t).wait_send()
        return carry

    lax.fori_loop(1, nx, drain_rs, 0)
    for copy, goes, comes in sends:
        @pl.when(comes)
        def _():
            copy().wait_recv()
    lat_ref[...] = lat[...]
    for copy, goes, comes in sends:
        @pl.when(goes)
        def _():
            copy().wait_send()
    out.wait()


def transformer_part(queries, attn_keys, attn_values, residual, out_weight, out_gate,
                     head_shift, head_scale, head_weight, head_bias):
    nx, nz = lax.axis_size("head"), lax.axis_size("seq") // 2
    frames, height, breadth, features = queries.shape
    model = residual.shape[3]
    rows, width = frames * height * breadth, features // nx
    heads = width // HEAD_DIM
    count = rows * nx
    share_cols = out_weight.shape[1]
    cells = head_weight.shape[1]
    there = pl.BlockSpec(memory_space=pltpu.HBM)
    vmem = pl.BlockSpec(memory_space=pltpu.VMEM)
    dma = pltpu.SemaphoreType.DMA
    bf, f32 = jnp.bfloat16, jnp.float32
    block = model // (2 * SUBS)
    return pl.pallas_call(
        functools.partial(block_kernel, nx, nz),
        out_shape=(jax.ShapeDtypeStruct((rows, model), bf), jax.ShapeDtypeStruct((2, 3, rows, 2 * cells), bf)),
        in_specs=[there] * 10,
        out_specs=(there, vmem),
        scratch_shapes=[
            pltpu.VMEM((count, width), bf),
            pltpu.VMEM((2, nz, count, width), bf),
            pltpu.VMEM((2, nz, count, width), bf),
            pltpu.VMEM((nz, 2, share_cols, width), bf),
            pltpu.VMEM((heads, HEAD_DIM, count), bf),
            pltpu.VMEM((heads, HEAD_DIM, count), f32),
            pltpu.VMEM((heads, 2, 1, count), f32),
            pltpu.VMEM((count, model), f32),
            pltpu.VMEM((2 * SUBS, nx, rows, block), bf),
            pltpu.VMEM((2 * SUBS, nx, rows, block), bf),
            pltpu.VMEM((count, width), bf),
            pltpu.VMEM((rows, model), bf),
            pltpu.VMEM((2, 3, rows, 2 * cells), bf),
            pltpu.VMEM((rows, model), bf),
            pltpu.VMEM((1, model), f32),
            pltpu.VMEM((1, model), f32),
            pltpu.VMEM((1, model), f32),
            pltpu.VMEM((model, cells), bf),
            pltpu.VMEM((1, cells), f32),
            dma((10,)), dma((3,)), dma((3,)),
            dma((4, nz // 2 + 1)), dma((4, nz // 2 + 1)),
            dma((2, nz)), dma((2, nz)),
            dma((2, nz // 2 + 1)), dma((2, nz // 2 + 1)),
            dma((nz,)), dma((nz,)),
            dma((2 * SUBS, nx)), dma((2 * SUBS, nx)),
            dma((5,)), dma((5,)), dma((1,)),
        ],
        compiler_params=pltpu.CompilerParams(
            collective_id=0, has_side_effects=True, vmem_limit_bytes=56 * 2**20),
        cost_estimate=pl.CostEstimate(flops=4 * count * count * 2 * nz * width, bytes_accessed=2**21, transcendentals=0),
        name="block_ring",
    )(queries.reshape(rows, features), attn_keys.reshape(rows, features), attn_values.reshape(rows, features),
      out_weight.T, residual.reshape(rows, model), out_gate.reshape(1, model), head_shift.reshape(1, model),
      head_scale.reshape(1, model), head_weight, head_bias.reshape(1, cells))


def on_device(queries, attn_keys, attn_values, residual, out_weight, out_gate, head_shift, head_scale,
              head_weight, head_bias, conv_weight, conv_bias, norm_gain):
    frames, height, breadth = queries.shape[:3]
    channels = head_weight.shape[1] // 4
    hidden, lat = transformer_part(queries, attn_keys, attn_values, residual, out_weight, out_gate,
                                   head_shift, head_scale, head_weight, head_bias)
    cells = lat[..., : 4 * channels].reshape(2, 3, frames, breadth, 2, 2, channels)
    video = cells.transpose(0, 2, 1, 4, 3, 5, 6).reshape(2 * frames, 6, 2 * breadth, channels)[:, 1:5]
    padded = jnp.pad(video, ((0, 0), (0, 0), (1, 1), (0, 0)))
    features = convolve(padded, frames, conv_weight, conv_bias, norm_gain)
    return hidden.reshape(residual.shape), features


def solution(mesh):
    return jax.shard_map(
        on_device,
        mesh=mesh,
        in_specs=(
            P(("clip", "head"), "seq", None, None),
            P(("clip", "head"), "seq", None, None),
            P(("clip", "head"), "seq", None, None),
            P(("clip", "head"), "seq", None, None),
            P("head", "seq"),
            P(),
            P(),
            P(),
            P(),
            P(),
            P(),
            P(),
            P(),
        ),
        out_specs=(P(("clip", "head"), "seq", None, None), P(("clip", "head"), "seq", None, None)),
        check_vma=False,
    )
```

time: 226 us -> 190 us (0.84)
  waiting for transfers between devices: 43.5 us -> 0 us
  Pallas kernels: 143 us -> 183 us
  between operations: 14.3 us -> 0.73 us
  starting transfers between devices: 13.2 us -> 0 us
  matrix products: 5.85 us -> 0.31 us
  local copies, waits for them, and re-layouts: 3.42 us -> 5.73 us
    pallas_call x1, Pallas kernels: 143 us -> 183 us  [transformer_part(): pl.pallas_call(functools.partial(block_kernel, nx, nz), out_shape=(jax.Sh...]
    reduce_scatter x1 -> x0, waiting for transfers between devices: 38.4 us -> none  [on_device(): lax.psum_scatter(partial_value.astype(jnp.bfloat16), 'head', scatter_dime...]
    ppermute x3 -> x0, starting transfers between devices: 13.1 us -> none  [the longest x1 8.43 us: padded_2(): before = lax.ppermute(last, axis, up)]
    dot_general x2 -> x0, matrix products: 5.54 us -> none  [the longest x1 5.23 us: on_device(): jnp.dot(attended, lax.all_gather(out_weight, 'seq', axis=1, tiled=True),...]
    ppermute x3 -> x0, waiting for transfers between devices: 4.28 us -> none  [the longest x1 3.28 us: padded_2(): after = lax.ppermute(first, axis, down)]
  transfers between devices with their start and end apart: 5 -> 0, of which waited for: 3 -> 0; matrix products, arithmetic and copies ran while one was open for 0% -> 0% of each run, Pallas kernels for 63% -> 0%
where the time goes in v2:
time: 190 us
  Pallas kernels  183 us (96%)
  local copies, waits for them, and re-layouts  5.73 us (3%)
    pallas_call x1, Pallas kernels, transformer_part(): pl.pallas_call(functools.partial(block_kernel, nx, nz), out_shape=(jax.Sh...  183 us
    unnamed x10, local copies, waits for them, and re-layouts  4.1 us

profile of v2, /device:TPU:65, one launch (start us, length us, event | category | flops | bytes accessed | tf_op | source)
XLA Modules:
  0.0 190.1 jit_solution(6328980359046383527)
XLA Ops:
  0.6 0.0 copy-start
  0.6 1.0 copy-done
  1.6 2.3 %copy.17.hw_in = bf16[5120,64]{1,0:T(8,128)(2,1)} copy(bf16[5120,64]{0,1:T(8,128)(2,1)} %param.21) | data formatting | bytes 1310720 | tf_op args[8]
  3.9 182.6 %block_ring.1 = (bf16[32,5120]{1,0:T(8,128)(2,1)}, bf16[2,3,32,128]{3,2,1,0:T(8,128)(2,1)}) custom-call(bf16[32,3072]{1,0:T(8,128)(2,1)} %bitcast.31, bf16[32,3072]{1,0:T(8,128)(2,1)} %bitcast.32, bf16[32,3072]{1,0:T(8,128)(2,1)} %bitcast.33, bf16[160,384]{1,0:T(8,128)(2,1)} %bitcast.34, bf16[32,5120]{1,0:T(8,128)(2,1)} %bitcast.30, f32[1,5120]{1,0:T(1,128)} %bitcast.35, ...), custom_call_target="tpu_custom_call" | custom-call | flops 3221225472 | bytes 2097152 | tf_op jit(solution)/shard_map/block_ring/pallas_call | solution.py:339
  186.5 0.9 reshape.65
  187.4 0.2 copy.18
  187.6 0.0 copy-start.2
  187.7 0.0 copy-start.3
  187.7 0.0 copy-start.1
  187.7 0.1 pad_slice_fusion
  187.9 0.3 concatenate.3
  188.2 0.1 copy-done.2
  188.3 0.3 multiply_reduce_fusion
  188.6 0.0 copy-done.3
  188.6 0.8 multiply_convert_fusion
  189.4 0.0 copy-done.1
  189.4 0.7 copy.21
  (3 shorter events, 0.1 us)
Async XLA Ops:
  0.6 1.0 copy-start
  187.6 0.7 copy-start.2
  187.7 0.9 copy-start.3
  187.7 1.7 copy-start.1

commit v3 on v2

--- a/solution.py
+++ b/solution.py
@@ -39,181 +39,314 @@
 
 def block_kernel(nx, nz, q_in, k_in, v_in, w_in, res_in, gate_in, shift_in, scale_in, hw_in, hb_in,
                  hidden_ref, lat_ref,
-                 qbuf, kbuf, vbuf, wbuf, qt, acc, stat, part, sums_out, sums_in, tokens, owned, lat,
+                 qa, ka, va, qp, kp, vp, wbuf, qt, acc, stat, part, sums_out, sums_in, tokens, plane_out, owned, lat,
                  res, gate, shift, gain, hw, hb,
                  local_sem, a2a_send, a2a_recv, ring_send, ring_recv, pair_send, pair_recv,
+                 pring_send, pring_recv, ppair_send, ppair_recv, back_send, back_recv,
                  w_send, w_recv, wpair_send, wpair_recv, rs_send, rs_recv, halo_send, halo_recv, out_sem):
     x = lax.axis_index("head")
     s = lax.axis_index("seq")
     z, c = s // 2, lax.rem(s, 2)
     nseq = 2 * nz
-    rows, width = k_in.shape[0], kbuf.shape[3]
-    heads = width // HEAD_DIM
+    rows, width = k_in.shape[0], tokens.shape[1]
     scale = HEAD_DIM ** (-0.5)
-    half = nz // 2
+    halfz, halfx = nz // 2, nx // 2
     features = part.shape[1]
+    queries = qt.shape[2]
+
+    def away(value, by, size):
+        return lax.rem(value + by + 2 * size, size)
 
     def seq_of(zz, cc):
-        return lax.rem(zz + 2 * nz, nz) * 2 + cc
+        return away(zz, 0, nz) * 2 + cc
 
     def remote(src, dst, send, recv, **where):
         return pltpu.make_async_remote_copy(
             src_ref=src, dst_ref=dst, send_sem=send, recv_sem=recv, device_id=where, device_id_type=MESH)
 
-    own_rows = pl.ds(pl.multiple_of(x * rows, rows), rows)
-    own_cols = pl.ds(pl.multiple_of(x * width, width), width)
-    mine = (kbuf.at[c, z], vbuf.at[c, z], qbuf)
+    def span(i, size):
+        return pl.ds(pl.multiple_of(i * size, size), size)
+
+    def column_head(xx):
+        return span(xx * (width // HEAD_DIM), HEAD_DIM)
+
+    def plane_head(zz):
+        return span((zz // 2) * (width // HEAD_DIM) + 1 + lax.rem(zz, 2), HEAD_DIM)
+
     ins = (k_in, v_in, q_in)
-    loads = [pltpu.make_async_copy(ins[i].at[:, own_cols], mine[i].at[own_rows, :], local_sem.at[i]) for i in range(3)]
-    loads.append(pltpu.make_async_copy(w_in, wbuf.at[z, c], local_sem.at[3]))
+    col_dst = (ka.at[c, z], va.at[c, z], qa)
+    plane_dst = (kp.at[c, x], vp.at[c, x], qp)
+    loads = [pltpu.make_async_copy(ins[i].at[:, column_head(x)], col_dst[i].at[span(x, rows), :], local_sem.at[i])
+             for i in range(3)]
+    loads += [pltpu.make_async_copy(ins[i].at[:, plane_head(z)], plane_dst[i].at[span(z, rows), :], local_sem.at[3 + i])
+              for i in range(3)]
+    w_load = pltpu.make_async_copy(w_in, wbuf.at[z, c], local_sem.at[6])
     late = ((res_in, res), (gate_in, gate), (shift_in, shift), (scale_in, gain), (hw_in, hw), (hb_in, hb))
-    loads += [pltpu.make_async_copy(a, b, local_sem.at[4 + i]) for i, (a, b) in enumerate(late)]
-    for load in loads:
+    late = [pltpu.make_async_copy(a, b, local_sem.at[7 + i]) for i, (a, b) in enumerate(late)]
+    for load in loads + [w_load] + late:
         load.start()
-
-    def away(value, by, size):
-        return lax.rem(value + by + size, size)
-
     lat[...] = jnp.zeros_like(lat)
+
+    alone = (z // 2 == x).astype(jnp.int32)
     barrier = pltpu.get_barrier_semaphore()
+
+    def greet(**where):
+        pl.semaphore_signal(barrier, inc=1, device_id=where, device_id_type=MESH)
+
     for d in range(1, nx):
-        pl.semaphore_signal(barrier, inc=1, device_id={"head": away(x, d, nx)}, device_id_type=MESH)
-    for other in (seq_of(z + 1, c), seq_of(z - 1, c), seq_of(z, 1 - c), away(s, 2 * c - 1, nseq)):
-        pl.semaphore_signal(barrier, inc=1, device_id={"seq": other}, device_id_type=MESH)
+        greet(head=away(x, d, nx))
+    for d in range(1, nz):
+        greet(seq=seq_of(z + d, c))
+    for other in (seq_of(z, 1 - c), away(s, 2 * c - 1, nseq)):
+        greet(seq=other)
     for dx in (1, -1):
         for ds in (1, -1):
-            pl.semaphore_signal(barrier, inc=1, device_id={"head": away(x, dx, nx), "seq": away(s, ds, nseq)},
-                                device_id_type=MESH)
-    pl.semaphore_wait(barrier, nx + 7)
+            greet(head=away(x, dx, nx), seq=away(s, ds, nseq))
+    for xx in range(nx):
+        for half in range(2):
+            @pl.when(jnp.logical_or(x != xx, z != 2 * x + half))
+            def _():
+                greet(head=xx, seq=seq_of(2 * x + half, c))
+    pl.semaphore_wait(barrier, nx - 1 + nz - 1 + 2 + 4 + 2 * nx - alone)
+
+    def far_first(size):
+        return sorted(range(1, size), key=lambda d: -min(d, size - d))
+
+    def exchange(i):
+        for d in far_first(nz):
+            to = away(z, d, nz)
+            remote(ins[i].at[:, plane_head(to)], plane_dst[i].at[span(z, rows), :],
+                   a2a_send.at[3 + i], a2a_recv.at[3 + i], seq=seq_of(to, c)).start()
+        for d in far_first(nx):
+            to = away(x, d, nx)
+            remote(ins[i].at[:, column_head(to)], col_dst[i].at[span(x, rows), :],
+                   a2a_send.at[i], a2a_recv.at[i], head=to).start()
 
     for i in range(3):
-        for d in range(1, nx):
-            peer = lax.rem(x + (d + 1) // 2 if d % 2 else x + nx - d // 2, nx)
-            cols = pl.ds(pl.multiple_of(peer * width, width), width)
-            remote(ins[i].at[:, cols], mine[i].at[own_rows, :], a2a_send.at[i], a2a_recv.at[i], head=peer).start()
-
-    def all_but_one(i):
-        piece = mine[i].at[pl.ds(0, rows * (nx - 1)), :]
+        exchange(i)
+
+    def from_column(i):
+        piece = col_dst[i].at[pl.ds(0, rows * (nx - 1)), :]
         return remote(piece, piece, a2a_send.at[i], a2a_recv.at[i], head=away(x, 1, nx))
 
-    bufs = (kbuf, vbuf)
+    def from_plane(i):
+        piece = plane_dst[i].at[pl.ds(0, rows * (nz - 1)), :]
+        return remote(piece, piece, a2a_send.at[3 + i], a2a_recv.at[3 + i], seq=seq_of(z + 1, c))
+
+    col_kv, plane_kv = (ka, va), (kp, vp)
+
+    def flow_of(kv, direction):
+        return 2 * kv + (1 if direction > 0 else 0)
 
     def hop(kv, direction, step, back):
-        slot = bufs[kv].at[c, lax.rem(z - direction * back + 2 * nz, nz)]
-        flow = 2 * kv + (1 if direction > 0 else 0)
+        slot, flow = col_kv[kv].at[c, away(z, -direction * back, nz)], flow_of(kv, direction)
         return remote(slot, slot, ring_send.at[flow, step], ring_recv.at[flow, step], seq=seq_of(z + direction, c))
 
+    def share(kv, zz, cc):
+        slot = col_kv[kv].at[cc, zz]
+        return remote(slot, slot, pair_send.at[kv, zz], pair_recv.at[kv, zz], seq=seq_of(z, 1 - c))
+
+    def phop(kv, direction, step, back):
+        slot, flow = plane_kv[kv].at[c, away(x, -direction * back, nx)], flow_of(kv, direction)
+        return remote(slot, slot, pring_send.at[flow, step], pring_recv.at[flow, step], head=away(x, direction, nx))
+
+    def pshare(kv, xx, cc):
+        slot = plane_kv[kv].at[cc, xx]
+        return remote(slot, slot, ppair_send.at[kv, xx], ppair_recv.at[kv, xx], seq=seq_of(z, 1 - c))
+
     def w_hop(direction, step, back):
-        slot = wbuf.at[lax.rem(z - direction * back + 2 * nz, nz), c]
-        flow = 1 if direction > 0 else 0
+        slot, flow = wbuf.at[away(z, -direction * back, nz), c], 1 if direction > 0 else 0
         return remote(slot, slot, w_send.at[flow, step], w_recv.at[flow, step], seq=seq_of(z + direction, c))
-
-    def share(kv, zz, cc):
-        slot = bufs[kv].at[cc, zz]
-        return remote(slot, slot, pair_send.at[kv, zz], pair_recv.at[kv, zz], seq=seq_of(z, 1 - c))
 
     def w_share(zz, cc):
         slot = wbuf.at[zz, cc]
         return remote(slot, slot, wpair_send.at[zz], wpair_recv.at[zz], seq=seq_of(z, 1 - c))
 
-    loads[3].wait()
+    def last_hop(kv, direction, half):
+        return half if (kv == 0) == (direction > 0) else half - 1
+
+    def w_last(direction):
+        return halfz if direction > 0 else halfz - 1
+
+    def w_step(h):
+        for direction in (1, -1):
+            @pl.when(h <= w_last(direction))
+            def _():
+                w_hop(direction, h, h).wait_recv()
+
+                @pl.when(h < w_last(direction))
+                def _():
+                    w_hop(direction, h + 1, h).start()
+
+                w_share(away(z, -direction * h, nz), c).start()
+
+    def col_step(h):
+        for kv in range(2):
+            for direction in (1, -1):
+                @pl.when(h <= last_hop(kv, direction, halfz))
+                def _():
+                    hop(kv, direction, h, h).wait_recv()
+
+                    @pl.when(h < last_hop(kv, direction, halfz))
+                    def _():
+                        hop(kv, direction, h + 1, h).start()
+
+                    share(kv, away(z, -direction * h, nz), c).start()
+
+    def plane_step(h):
+        for kv in range(2):
+            for direction in (1, -1):
+                @pl.when(h <= last_hop(kv, direction, halfx))
+                def _():
+                    phop(kv, direction, h, h).wait_recv()
+
+                    @pl.when(h < last_hop(kv, direction, halfx))
+                    def _():
+                        phop(kv, direction, h + 1, h).start()
+
+                    pshare(kv, away(x, -direction * h, nx), c).start()
+
+    def fold(j, keys, values):
+        scores = [lax.dot_general(key[...], qt[j], (((1,), (0,)), ((), ())), preferred_element_type=jnp.float32)
+                  for key in keys]
+        before = stat[j, 0]
+        peak = before
+        for part_scores in scores:
+            peak = jnp.maximum(peak, jnp.max(part_scores, 0, keepdims=True))
+        factor = jnp.exp((before - peak) * scale)
+        total, product = stat[j, 1] * factor, acc[j] * factor
+        for part_scores, value in zip(scores, values):
+            weights = jnp.exp((part_scores - peak) * scale)
+            total = total + jnp.sum(weights, 0, keepdims=True)
+            product = product + lax.dot_general(value[...], weights.astype(jnp.bfloat16), (((0,), (0,)), ((), ())),
+                                                preferred_element_type=jnp.float32)
+        stat[j, 0], stat[j, 1], acc[j] = peak, total, product
+
+    def col_attend(zs):
+        for zz in zs:
+            for kv in range(2):
+                share(kv, zz, 1 - c).wait_recv()
+        fold(0, [ka.at[lane, zz] for zz in zs for lane in range(2)], [va.at[lane, zz] for zz in zs for lane in range(2)])
+
+    def col_attend_at(h):
+        col_attend([away(z, -h, nz), away(z, h, nz)])
+
+    def plane_attend(xx):
+        for kv in range(2):
+            pshare(kv, xx, 1 - c).wait_recv()
+
+        def part_of_queries(j, carry):
+            fold(j, [kp.at[lane, xx] for lane in range(2)], [vp.at[lane, xx] for lane in range(2)])
+            return carry
+
+        lax.fori_loop(1, qt.shape[0], part_of_queries, 0)
+
+    def plane_attend_at(h):
+        def side(i, carry):
+            plane_attend(away(x, (2 * i - 1) * h, nx))
+            return carry
+
+        lax.fori_loop(0, 2, side, 0)
+
+    w_load.wait()
     for direction in (1, -1):
         w_hop(direction, 1, 0).start()
     w_share(z, c).start()
     for kv in range(2):
+        loads[3 + kv].wait()
+        from_plane(kv).wait_recv()
+        for direction in (1, -1):
+            if last_hop(kv, direction, halfx) >= 1:
+                phop(kv, direction, 1, 0).start()
+        pshare(kv, x, c).start()
+    for kv in range(2):
         loads[kv].wait()
-        all_but_one(kv).wait_recv()
+        from_column(kv).wait_recv()
         for direction in (1, -1):
             hop(kv, direction, 1, 0).start()
         share(kv, z, c).start()
-    loads[2].wait()
-    all_but_one(2).wait_recv()
-
-    for j in range(heads):
-        qt[j] = qbuf[:, j * HEAD_DIM:(j + 1) * HEAD_DIM].astype(jnp.float32).T.astype(jnp.bfloat16)
+    for i, dst in ((2, qa), (5, qp)):
+        loads[i].wait()
+    from_column(2).wait_recv()
+    from_plane(2).wait_recv()
+    w_step(1)
+
     acc[...] = jnp.zeros_like(acc)
     stat[:, 0] = jnp.full(stat[:, 0].shape, -1e30, jnp.float32)
     stat[:, 1] = jnp.zeros_like(stat[:, 1])
-
-    def attend(lane, zz):
-        for j in range(heads):
-            cols = pl.ds(j * HEAD_DIM, HEAD_DIM)
-            scores = lax.dot_general(kbuf[lane, zz, :, cols], qt[j], (((1,), (0,)), ((), ())),
-                                     preferred_element_type=jnp.float32)
-            before = stat[j, 0]
-            peak = jnp.maximum(before, jnp.max(scores, 0, keepdims=True))
-            factor = jnp.exp((before - peak) * scale)
-            weights = jnp.exp((scores - peak) * scale)
-            stat[j, 1] = stat[j, 1] * factor + jnp.sum(weights, 0, keepdims=True)
-            stat[j, 0] = peak
-            acc[j] = acc[j] * factor + lax.dot_general(
-                vbuf[lane, zz, :, cols], weights.astype(jnp.bfloat16), (((0,), (0,)), ((), ())),
-                preferred_element_type=jnp.float32)
-
-    def last_hop(kv, direction):
-        return half if (kv == 0) == (direction > 0) else half - 1
-
-    def w_last(direction):
-        return half if direction > 0 else half - 1
-
-    def both_lanes(zz):
-        attend(c, zz)
-        for kv in range(2):
-            share(kv, zz, 1 - c).wait_recv()
-        attend(1 - c, zz)
-
-    both_lanes(z)
-
-    def step(h, carry):
-        for kv in range(2):
-            for direction in (1, -1):
-                hop(kv, direction, h, h).wait_recv()
-
-                @pl.when(h < last_hop(kv, direction))
-                def _():
-                    hop(kv, direction, h + 1, h).start()
-
-                share(kv, lax.rem(z - direction * h + nz, nz), c).start()
-        for direction in (1, -1):
-            w_hop(direction, h, h).wait_recv()
-
-            @pl.when(h < w_last(direction))
-            def _():
-                w_hop(direction, h + 1, h).start()
-
-            w_share(lax.rem(z - direction * h + nz, nz), c).start()
-
-        def block(i, carry):
-            both_lanes(lax.rem(z - (1 - 2 * i) * h + nz, nz))
-            return carry
-
-        lax.fori_loop(0, 2, block, 0)
-        return carry
-
-    lax.fori_loop(1, half, step, 0)
-    far = lax.rem(z + half, nz)
-    for kv in range(2):
-        hop(kv, 1 if kv == 0 else -1, half, half).wait_recv()
-        share(kv, far, c).start()
-    w_hop(1, half, half).wait_recv()
-    w_share(far, c).start()
-    both_lanes(far)
-
-    for j in range(heads):
-        tokens[:, j * HEAD_DIM:(j + 1) * HEAD_DIM] = (acc[j] / stat[j, 1]).T.astype(jnp.bfloat16)
+    qt[0] = qa[...].astype(jnp.float32).T.astype(jnp.bfloat16)
+    for j in range(1, qt.shape[0]):
+        qt[j] = qp[(j - 1) * queries:j * queries, :].astype(jnp.float32).T.astype(jnp.bfloat16)
+    col_attend([z])
+    plane_attend(x)
+    w_step(2)
+
+    def step(i, carry):
+        col_step(2 * i - 1)
+
+        @pl.when(i > 1)
+        def _():
+            col_attend_at(2 * i - 2)
+
+        plane_step(i)
+        col_step(2 * i)
+        col_attend_at(2 * i - 1)
+        w_step(i + 2)
+        plane_attend_at(i)
+        return carry
+
+    lax.fori_loop(1, halfx, step, 0)
+    col_step(halfz - 1)
+    if halfz > 2:
+        col_attend_at(halfz - 2)
+    plane_step(halfx)
+    plane_attend(away(x, halfx, nx))
+
+    for j in range(1, qt.shape[0]):
+        plane_out[(j - 1) * queries:j * queries, :] = (acc[j] / stat[j, 1]).T.astype(jnp.bfloat16)
+    group, which = z // 2, lax.rem(z, 2)
+
+    def back(zz, xx, part_of):
+        return remote(plane_out.at[span(zz, rows), :], tokens.at[span(xx, rows), span(1 + part_of, HEAD_DIM)],
+                      back_send.at[zz], back_recv.at[2 * xx + part_of], head=group, seq=seq_of(zz, c))
+
+    for d in far_first(nz) + [0]:
+        zz = away(z, d, nz)
+        if d:
+            back(zz, x, which).start()
+        else:
+            @pl.when(alone == 0)
+            def _():
+                back(zz, x, which).start()
+
+            @pl.when(alone == 1)
+            def _():
+                tokens[span(x, rows), span(1 + which, HEAD_DIM)] = plane_out[span(zz, rows), :]
+
+    col_step(halfz)
+    col_attend_at(halfz - 1)
+    col_attend([away(z, halfz, nz)])
+    tokens[:, 0:HEAD_DIM] = (acc[0] / stat[0, 1]).T.astype(jnp.bfloat16)
+    for h in range(halfx + 2, halfz + 1):
+        w_step(h)
 
     def w_land(zz, carry):
         w_share(zz, 1 - c).wait_recv()
         return carry
 
     lax.fori_loop(0, nz, w_land, 0)
+    for xx in range(nx):
+        for part_of in range(2):
+            @pl.when(jnp.logical_or(alone == 0, jnp.logical_or(x != xx, which != part_of)))
+            def _():
+                back(z, xx, part_of).wait_recv()
 
     w_rows = w_in.shape[0]
     tile = 4 * w_rows
 
     def project(i, carry):
         columns = wbuf[pl.ds(2 * i, 2)].reshape(tile, width)
-        part[:, pl.ds(pl.multiple_of(i * tile, tile), tile)] = lax.dot_general(
+        part[:, span(i, tile)] = lax.dot_general(
             tokens[...], columns, (((1,), (1,)), ((), ())), preferred_element_type=jnp.float32)
         return carry
 
@@ -221,8 +354,8 @@
     block = features // (2 * SUBS)
 
     def term(flow, direction, t):
-        owner = lax.rem(x - direction * t + 2 * nx, nx)
-        return part[pl.ds(pl.multiple_of(owner * rows, rows), rows), flow * block:(flow + 1) * block]
+        owner = away(x, -direction * t, nx)
+        return part[span(owner, rows), flow * block:(flow + 1) * block]
 
     def rs(flow, direction, t):
         return remote(sums_out.at[flow, t], sums_in.at[flow, t], rs_send.at[flow, t], rs_recv.at[flow, t],
@@ -242,7 +375,7 @@
         return carry
 
     lax.fori_loop(2, nx, rs_step, 0)
-    for load in loads[4:]:
+    for load in late:
         load.wait()
     for f, direction in flows:
         rs(f, direction, nx - 1).wait_recv()
@@ -279,26 +412,39 @@
             copy().start()
 
     for i in range(3):
-        all_but_one(i).wait_send()
+        from_column(i).wait_send()
+        from_plane(i).wait_send()
 
     def drain(h, carry):
         for kv in range(2):
             for direction in (1, -1):
-                @pl.when(h <= last_hop(kv, direction))
+                @pl.when(h <= last_hop(kv, direction, halfz))
                 def _():
                     hop(kv, direction, h, h - 1).wait_send()
+
+                @pl.when(h <= last_hop(kv, direction, halfx))
+                def _():
+                    phop(kv, direction, h, h - 1).wait_send()
         for direction in (1, -1):
             @pl.when(h <= w_last(direction))
             def _():
                 w_hop(direction, h, h - 1).wait_send()
         return carry
 
-    lax.fori_loop(1, half + 1, drain, 0)
+    lax.fori_loop(1, halfz + 1, drain, 0)
 
     def drain_pair(zz, carry):
         for kv in range(2):
             share(kv, zz, c).wait_send()
+
+            @pl.when(zz < nx)
+            def _():
+                pshare(kv, zz, c).wait_send()
         w_share(zz, c).wait_send()
+
+        @pl.when(jnp.logical_or(alone == 0, zz != z))
+        def _():
+            back(zz, x, which).wait_send()
         return carry
 
     lax.fori_loop(0, nz, drain_pair, 0)
@@ -329,7 +475,10 @@
     rows, width = frames * height * breadth, features // nx
     heads = width // HEAD_DIM
     count = rows * nx
+    planes = rows * nz
     share_cols = out_weight.shape[1]
+    if nz != 2 * nx or heads != 3:
+        raise ValueError("unsupported mesh")
     cells = head_weight.shape[1]
     there = pl.BlockSpec(memory_space=pltpu.HBM)
     vmem = pl.BlockSpec(memory_space=pltpu.VMEM)
@@ -342,9 +491,12 @@
         in_specs=[there] * 10,
         out_specs=(there, vmem),
         scratch_shapes=[
-            pltpu.VMEM((count, width), bf),
-            pltpu.VMEM((2, nz, count, width), bf),
-            pltpu.VMEM((2, nz, count, width), bf),
+            pltpu.VMEM((count, HEAD_DIM), bf),
+            pltpu.VMEM((2, nz, count, HEAD_DIM), bf),
+            pltpu.VMEM((2, nz, count, HEAD_DIM), bf),
+            pltpu.VMEM((planes, HEAD_DIM), bf),
+            pltpu.VMEM((2, nx, planes, HEAD_DIM), bf),
+            pltpu.VMEM((2, nx, planes, HEAD_DIM), bf),
             pltpu.VMEM((nz, 2, share_cols, width), bf),
             pltpu.VMEM((heads, HEAD_DIM, count), bf),
             pltpu.VMEM((heads, HEAD_DIM, count), f32),
@@ -353,6 +505,7 @@
             pltpu.VMEM((2 * SUBS, nx, rows, block), bf),
             pltpu.VMEM((2 * SUBS, nx, rows, block), bf),
             pltpu.VMEM((count, width), bf),
+            pltpu.VMEM((planes, HEAD_DIM), bf),
             pltpu.VMEM((rows, model), bf),
             pltpu.VMEM((2, 3, rows, 2 * cells), bf),
             pltpu.VMEM((rows, model), bf),
@@ -361,9 +514,12 @@
             pltpu.VMEM((1, model), f32),
             pltpu.VMEM((model, cells), bf),
             pltpu.VMEM((1, cells), f32),
-            dma((10,)), dma((3,)), dma((3,)),
+            dma((13,)), dma((6,)), dma((6,)),
             dma((4, nz // 2 + 1)), dma((4, nz // 2 + 1)),
             dma((2, nz)), dma((2, nz)),
+            dma((4, nx // 2 + 1)), dma((4, nx // 2 + 1)),
+            dma((2, nx)), dma((2, nx)),
+            dma((nz,)), dma((2 * nx,)),
             dma((2, nz // 2 + 1)), dma((2, nz // 2 + 1)),
             dma((nz,)), dma((nz,)),
             dma((2 * SUBS, nx)), dma((2 * SUBS, nx)),

time: 190 us -> 177 us (0.932)
  Pallas kernels: 183 us -> 169 us
    pallas_call x1, Pallas kernels: 183 us -> 169 us  [transformer_part(): pl.pallas_call(functools.partial(block_kernel, nx, nz), out_shape=(jax.Sh...]
where the time goes in v3:
time: 177 us; the launch traced here: 176 us
  Pallas kernels  169 us (95%)
  local copies, waits for them, and re-layouts  5.73 us (3%)
    pallas_call x1, Pallas kernels, transformer_part(): pl.pallas_call(functools.partial(block_kernel, nx, nz), out_shape=(jax.Sh...  169 us
    unnamed x10, local copies, waits for them, and re-layouts  4.1 us

profile of v3, /device:TPU:65, one launch (start us, length us, event | category | flops | bytes accessed | tf_op | source)
XLA Modules:
  0.0 176.4 jit_solution(12156848604522910259)
XLA Ops:
  0.6 0.0 copy-start
  0.6 1.0 copy-done
  1.6 2.3 %copy.17.hw_in = bf16[5120,64]{1,0:T(8,128)(2,1)} copy(bf16[5120,64]{0,1:T(8,128)(2,1)} %param.21) | data formatting | bytes 1310720 | tf_op args[8]
  3.9 168.8 %block_ring.1 = (bf16[32,5120]{1,0:T(8,128)(2,1)}, bf16[2,3,32,128]{3,2,1,0:T(8,128)(2,1)}) custom-call(bf16[32,3072]{1,0:T(8,128)(2,1)} %bitcast.31, bf16[32,3072]{1,0:T(8,128)(2,1)} %bitcast.32, bf16[32,3072]{1,0:T(8,128)(2,1)} %bitcast.33, bf16[160,384]{1,0:T(8,128)(2,1)} %bitcast.34, bf16[32,5120]{1,0:T(8,128)(2,1)} %bitcast.30, f32[1,5120]{1,0:T(1,128)} %bitcast.35, ...), custom_call_target="tpu_custom_call" | custom-call | flops 3221225472 | bytes 2097152 | tf_op jit(solution)/shard_map/block_ring/pallas_call | solution.py:488
  172.8 0.9 reshape.65
  173.7 0.2 copy.18
  173.9 0.0 copy-start.2
  174.0 0.0 copy-start.3
  174.0 0.0 copy-start.1
  174.0 0.1 pad_slice_fusion
  174.1 0.3 concatenate.3
  174.5 0.1 copy-done.2
  174.6 0.3 multiply_reduce_fusion
  174.9 0.0 copy-done.3
  174.9 0.8 multiply_convert_fusion
  175.7 0.0 copy-done.1
  175.7 0.7 copy.21
  (3 shorter events, 0.1 us)
Async XLA Ops:
  0.6 1.0 copy-start
  173.9 0.7 copy-start.2
  174.0 0.9 copy-start.3
  174.0 1.7 copy-start.1

commit v4 on v3

--- a/solution.py
+++ b/solution.py
@@ -9,7 +9,6 @@
 
 HEAD_DIM = 128
 MESH = pl.DeviceIdType.MESH
-SUBS = 2
 
 
 def convolve(padded, frames, conv_weight, conv_bias, norm_gain):
@@ -49,9 +48,8 @@
     z, c = s // 2, lax.rem(s, 2)
     nseq = 2 * nz
     rows, width = k_in.shape[0], tokens.shape[1]
-    scale = HEAD_DIM ** (-0.5)
+    scale = HEAD_DIM ** (-0.5) * 1.4426950408889634
     halfz, halfx = nz // 2, nx // 2
-    features = part.shape[1]
     queries = qt.shape[2]
 
     def away(value, by, size):
@@ -213,10 +211,10 @@
         peak = before
         for part_scores in scores:
             peak = jnp.maximum(peak, jnp.max(part_scores, 0, keepdims=True))
-        factor = jnp.exp((before - peak) * scale)
+        factor = jnp.exp2((before - peak) * scale)
         total, product = stat[j, 1] * factor, acc[j] * factor
         for part_scores, value in zip(scores, values):
-            weights = jnp.exp((part_scores - peak) * scale)
+            weights = jnp.exp2((part_scores - peak) * scale)
             total = total + jnp.sum(weights, 0, keepdims=True)
             product = product + lax.dot_general(value[...], weights.astype(jnp.bfloat16), (((0,), (0,)), ((), ())),
                                                 preferred_element_type=jnp.float32)
@@ -235,11 +233,8 @@
         for kv in range(2):
             pshare(kv, xx, 1 - c).wait_recv()
 
-        def part_of_queries(j, carry):
+        for j in range(1, qt.shape[0]):
             fold(j, [kp.at[lane, xx] for lane in range(2)], [vp.at[lane, xx] for lane in range(2)])
-            return carry
-
-        lax.fori_loop(1, qt.shape[0], part_of_queries, 0)
 
     def plane_attend_at(h):
         def side(i, carry):
@@ -280,6 +275,12 @@
     col_attend([z])
     plane_attend(x)
     w_step(2)
+    w_at = [2]
+
+    def w_reach(h):
+        while w_at[0] < min(h, halfz):
+            w_at[0] += 1
+            w_step(w_at[0])
 
     def step(i, carry):
         col_step(2 * i - 1)
@@ -291,12 +292,12 @@
         plane_step(i)
         col_step(2 * i)
         col_attend_at(2 * i - 1)
-        w_step(i + 2)
         plane_attend_at(i)
         return carry
 
     lax.fori_loop(1, halfx, step, 0)
     col_step(halfz - 1)
+    w_reach(3)
     if halfz > 2:
         col_attend_at(halfz - 2)
     plane_step(halfx)
@@ -323,65 +324,65 @@
             def _():
                 tokens[span(x, rows), span(1 + which, HEAD_DIM)] = plane_out[span(zz, rows), :]
 
+    w_reach(4)
     col_step(halfz)
     col_attend_at(halfz - 1)
     col_attend([away(z, halfz, nz)])
     tokens[:, 0:HEAD_DIM] = (acc[0] / stat[0, 1]).T.astype(jnp.bfloat16)
-    for h in range(halfx + 2, halfz + 1):
-        w_step(h)
-
-    def w_land(zz, carry):
-        w_share(zz, 1 - c).wait_recv()
-        return carry
-
-    lax.fori_loop(0, nz, w_land, 0)
+    w_reach(5)
     for xx in range(nx):
         for part_of in range(2):
             @pl.when(jnp.logical_or(alone == 0, jnp.logical_or(x != xx, which != part_of)))
             def _():
                 back(z, xx, part_of).wait_recv()
 
-    w_rows = w_in.shape[0]
-    tile = 4 * w_rows
-
-    def project(i, carry):
-        columns = wbuf[pl.ds(2 * i, 2)].reshape(tile, width)
-        part[:, span(i, tile)] = lax.dot_general(
+    tile = 4 * w_in.shape[0]
+    blocks = nz // 2
+    order = sorted(range(1 - (blocks + 1) // 2, blocks // 2 + 1), key=lambda k: (abs(k), -k))
+    flows = [(f, 1 if f % 2 == 0 else -1, away(z // 2, k, blocks)) for f, k in enumerate(order)]
+    groups = [flows[g:g + 2] for g in range(0, blocks, 2)]
+    reach = [max(min(2 * abs(order[f]) + 1, halfz) for f, _, _ in group) for group in groups]
+
+    def project(block):
+        for i in range(2):
+            w_share(2 * block + i, 1 - c).wait_recv()
+        columns = wbuf[pl.ds(2 * block, 2)].reshape(tile, width)
+        part[:, span(block, tile)] = lax.dot_general(
             tokens[...], columns, (((1,), (1,)), ((), ())), preferred_element_type=jnp.float32)
-        return carry
-
-    lax.fori_loop(0, nz // 2, project, 0)
-    block = features // (2 * SUBS)
-
-    def term(flow, direction, t):
-        owner = away(x, -direction * t, nx)
-        return part[span(owner, rows), flow * block:(flow + 1) * block]
-
-    def rs(flow, direction, t):
-        return remote(sums_out.at[flow, t], sums_in.at[flow, t], rs_send.at[flow, t], rs_recv.at[flow, t],
+
+    def term(direction, block, t):
+        return part[span(away(x, -direction * t, nx), rows), span(block, tile)]
+
+    def rs(f, direction, t):
+        return remote(sums_out.at[f, t], sums_in.at[f, t], rs_send.at[f, t], rs_recv.at[f, t],
                       head=away(x, direction, nx))
 
-    flows = [(f, 1 if f % 2 else -1) for f in range(2 * SUBS)]
-    for f, direction in flows:
-        sums_out[f, 1] = term(f, direction, 1).astype(jnp.bfloat16)
-    for f, direction in flows:
-        rs(f, direction, 1).start()
-
-    def rs_step(t, carry):
-        for f, direction in flows:
-            rs(f, direction, t - 1).wait_recv()
-            sums_out[f, t] = (sums_in[f, t - 1].astype(jnp.float32) + term(f, direction, t)).astype(jnp.bfloat16)
-            rs(f, direction, t).start()
-        return carry
-
-    lax.fori_loop(2, nx, rs_step, 0)
-    for load in late:
-        load.wait()
-    for f, direction in flows:
-        rs(f, direction, nx - 1).wait_recv()
-        cols = slice(f * block, (f + 1) * block)
-        total = sums_in[f, nx - 1].astype(jnp.float32) + term(f, direction, nx)
-        owned[:, cols] = (res[:, cols].astype(jnp.float32) + gate[:, cols] * total).astype(jnp.bfloat16)
+    for turn in range(nx + len(groups) - 1):
+        for g, group in enumerate(groups):
+            t = turn - g + 1
+            if t == 1:
+                w_reach(reach[g])
+                for f, direction, block in group:
+                    project(block)
+                for f, direction, block in group:
+                    sums_out[f, 1] = term(direction, block, 1).astype(jnp.bfloat16)
+                for f, direction, block in group:
+                    rs(f, direction, 1).start()
+            elif 1 < t < nx:
+                for f, direction, block in group:
+                    rs(f, direction, t - 1).wait_recv()
+                    sums_out[f, t] = (sums_in[f, t - 1].astype(jnp.float32) + term(direction, block, t)).astype(jnp.bfloat16)
+                    rs(f, direction, t).start()
+            elif t == nx:
+                if g == 0:
+                    for load in late:
+                        load.wait()
+                for f, direction, block in group:
+                    rs(f, direction, nx - 1).wait_recv()
+                    total = sums_in[f, nx - 1].astype(jnp.float32) + term(direction, block, nx)
+                    at = span(block, tile)
+                    owned[:, at] = (res[:, at].astype(jnp.float32) + gate[:, at] * total).astype(jnp.bfloat16)
+        w_reach(6 + turn)
 
     out = pltpu.make_async_copy(owned, hidden_ref, out_sem.at[0])
     out.start()
@@ -389,7 +390,7 @@
     center = values - jnp.mean(values, -1, keepdims=True)
     spread = jnp.mean(center * center, -1, keepdims=True)
     normed = (center * lax.rsqrt(spread + 1e-06) * (1.0 + gain[...]) + shift[...]).astype(jnp.bfloat16)
-    latent = jnp.dot(normed, hw[...], preferred_element_type=jnp.float32) + hb[...]
+    latent = lax.dot_general(normed, hw[...], (((1,), (1,)), ((), ())), preferred_element_type=jnp.float32) + hb[...]
     cells = latent.shape[1]
     lat[1, 1, :, 0:cells] = latent.astype(jnp.bfloat16)
 
@@ -450,7 +451,7 @@
     lax.fori_loop(0, nz, drain_pair, 0)
 
     def drain_rs(t, carry):
-        for f, direction in flows:
+        for f, direction, block in flows:
             rs(f, direction, t).wait_send()
         return carry
 
@@ -484,7 +485,7 @@
     vmem = pl.BlockSpec(memory_space=pltpu.VMEM)
     dma = pltpu.SemaphoreType.DMA
     bf, f32 = jnp.bfloat16, jnp.float32
-    block = model // (2 * SUBS)
+    tile = 4 * share_cols
     return pl.pallas_call(
         functools.partial(block_kernel, nx, nz),
         out_shape=(jax.ShapeDtypeStruct((rows, model), bf), jax.ShapeDtypeStruct((2, 3, rows, 2 * cells), bf)),
@@ -502,8 +503,8 @@
             pltpu.VMEM((heads, HEAD_DIM, count), f32),
             pltpu.VMEM((heads, 2, 1, count), f32),
             pltpu.VMEM((count, model), f32),
-            pltpu.VMEM((2 * SUBS, nx, rows, block), bf),
-            pltpu.VMEM((2 * SUBS, nx, rows, block), bf),
+            pltpu.VMEM((nz // 2, nx, rows, tile), bf),
+            pltpu.VMEM((nz // 2, nx, rows, tile), bf),
             pltpu.VMEM((count, width), bf),
             pltpu.VMEM((planes, HEAD_DIM), bf),
             pltpu.VMEM((rows, model), bf),
@@ -512,7 +513,7 @@
             pltpu.VMEM((1, model), f32),
             pltpu.VMEM((1, model), f32),
             pltpu.VMEM((1, model), f32),
-            pltpu.VMEM((model, cells), bf),
+            pltpu.VMEM((cells, model), bf),
             pltpu.VMEM((1, cells), f32),
             dma((13,)), dma((6,)), dma((6,)),
             dma((4, nz // 2 + 1)), dma((4, nz // 2 + 1)),
@@ -522,7 +523,7 @@
             dma((nz,)), dma((2 * nx,)),
             dma((2, nz // 2 + 1)), dma((2, nz // 2 + 1)),
             dma((nz,)), dma((nz,)),
-            dma((2 * SUBS, nx)), dma((2 * SUBS, nx)),
+            dma((nz // 2, nx)), dma((nz // 2, nx)),
             dma((5,)), dma((5,)), dma((1,)),
         ],
         compiler_params=pltpu.CompilerParams(
@@ -531,7 +532,7 @@
         name="block_ring",
     )(queries.reshape(rows, features), attn_keys.reshape(rows, features), attn_values.reshape(rows, features),
       out_weight.T, residual.reshape(rows, model), out_gate.reshape(1, model), head_shift.reshape(1, model),
-      head_scale.reshape(1, model), head_weight, head_bias.reshape(1, cells))
+      head_scale.reshape(1, model), head_weight.T, head_bias.reshape(1, cells))
 
 
 def on_device(queries, attn_keys, attn_values, residual, out_weight, out_gate, head_shift, head_scale,

time: 177 us -> 175 us (0.989)
    unnamed x10 -> x9, local copies, waits for them, and re-layouts: 4.1 us -> 2.69 us
where the time goes in v4:
time: 175 us
  Pallas kernels  169 us (97%)
  local copies, waits for them, and re-layouts  4.32 us (2%)
    pallas_call x1, Pallas kernels, transformer_part(): pl.pallas_call(functools.partial(block_kernel, nx, nz), out_shape=(jax.Sh...  169 us

profile of v4, /device:TPU:65, one launch (start us, length us, event | category | flops | bytes accessed | tf_op | source)
XLA Modules:
  0.0 174.8 jit_solution(4384581288147106724)
XLA Ops:
  0.6 0.0 copy-start
  0.6 1.0 copy-done
  1.6 168.7 %block_ring.1 = (bf16[32,5120]{1,0:T(8,128)(2,1)}, bf16[2,3,32,128]{3,2,1,0:T(8,128)(2,1)}) custom-call(bf16[32,3072]{1,0:T(8,128)(2,1)} %bitcast.33, bf16[32,3072]{1,0:T(8,128)(2,1)} %bitcast.34, bf16[32,3072]{1,0:T(8,128)(2,1)} %bitcast.35, bf16[160,384]{1,0:T(8,128)(2,1)} %bitcast.36, bf16[32,5120]{1,0:T(8,128)(2,1)} %bitcast.32, f32[1,5120]{1,0:T(1,128)} %bitcast.37, ...), custom_call_target="tpu_custom_call" | custom-call | flops 3221225472 | bytes 2097152 | tf_op jit(solution)/shard_map/block_ring/pallas_call | solution.py:489
  170.3 0.9 reshape.65
  171.2 0.2 copy.16
  171.5 0.1 pad_slice_fusion
  171.6 0.0 copy-start.2
  171.6 0.3 concatenate.3
  172.0 0.3 copy-done.2
  172.3 0.0 copy-start.1
  172.3 0.3 multiply_reduce_fusion
  172.6 0.0 copy-start.3
  172.6 0.7 copy-done.3
  173.3 0.8 multiply_convert_fusion
  174.1 0.0 copy-done.1
  174.1 0.7 copy.19
  (3 shorter events, 0.1 us)
Async XLA Ops:
  0.6 1.0 copy-start
  171.6 0.7 copy-start.2
  172.3 1.8 %copy-start.1 = (bf16[32,5120]{1,0:T(8,128)(2,1)S(1)}, bf16[32,5120]{1,0:T(8,128)(2,1)}, u32[]{:S(2)}) copy-start(bf16[32,5120]{1,0:T(8,128)(2,1)} %get-tuple-element.4) | copy-start | bytes 983044
  172.6 0.7 copy-start.3

commit v5 on v4

--- a/solution.py
+++ b/solution.py
@@ -178,8 +178,8 @@
 
                 w_share(away(z, -direction * h, nz), c).start()
 
-    def col_step(h):
-        for kv in range(2):
+    def col_step(h, kinds=(0, 1)):
+        for kv in kinds:
             for direction in (1, -1):
                 @pl.when(h <= last_hop(kv, direction, halfz))
                 def _():
@@ -235,13 +235,6 @@
 
         for j in range(1, qt.shape[0]):
             fold(j, [kp.at[lane, xx] for lane in range(2)], [vp.at[lane, xx] for lane in range(2)])
-
-    def plane_attend_at(h):
-        def side(i, carry):
-            plane_attend(away(x, (2 * i - 1) * h, nx))
-            return carry
-
-        lax.fori_loop(0, 2, side, 0)
 
     w_load.wait()
     for direction in (1, -1):
@@ -260,11 +253,13 @@
         for direction in (1, -1):
             hop(kv, direction, 1, 0).start()
         share(kv, z, c).start()
-    for i, dst in ((2, qa), (5, qp)):
+    w_step(1)
+    col_step(1)
+    for i in (2, 5):
         loads[i].wait()
     from_column(2).wait_recv()
     from_plane(2).wait_recv()
-    w_step(1)
+    plane_step(1)
 
     acc[...] = jnp.zeros_like(acc)
     stat[:, 0] = jnp.full(stat[:, 0].shape, -1e30, jnp.float32)
@@ -283,24 +278,19 @@
             w_step(w_at[0])
 
     def step(i, carry):
-        col_step(2 * i - 1)
-
-        @pl.when(i > 1)
-        def _():
-            col_attend_at(2 * i - 2)
-
-        plane_step(i)
-        col_step(2 * i)
+        col_step(2 * i, (0,))
         col_attend_at(2 * i - 1)
-        plane_attend_at(i)
+        col_step(2 * i, (1,))
+        plane_attend(away(x, -i, nx))
+        plane_step(i + 1)
+        col_step(2 * i + 1, (0,))
+        plane_attend(away(x, i, nx))
+        col_step(2 * i + 1, (1,))
+        col_attend_at(2 * i)
         return carry
 
     lax.fori_loop(1, halfx, step, 0)
-    col_step(halfz - 1)
     w_reach(3)
-    if halfz > 2:
-        col_attend_at(halfz - 2)
-    plane_step(halfx)
     plane_attend(away(x, halfx, nx))
 
     for j in range(1, qt.shape[0]):
@@ -324,9 +314,9 @@
             def _():
                 tokens[span(x, rows), span(1 + which, HEAD_DIM)] = plane_out[span(zz, rows), :]
 
-    w_reach(4)
     col_step(halfz)
     col_attend_at(halfz - 1)
+    w_reach(4)
     col_attend([away(z, halfz, nz)])
     tokens[:, 0:HEAD_DIM] = (acc[0] / stat[0, 1]).T.astype(jnp.bfloat16)
     w_reach(5)
@@ -339,9 +329,9 @@
     tile = 4 * w_in.shape[0]
     blocks = nz // 2
     order = sorted(range(1 - (blocks + 1) // 2, blocks // 2 + 1), key=lambda k: (abs(k), -k))
-    flows = [(f, 1 if f % 2 == 0 else -1, away(z // 2, k, blocks)) for f, k in enumerate(order)]
+    flows = [(f, away(z // 2, k, blocks)) for f, k in enumerate(order)]
     groups = [flows[g:g + 2] for g in range(0, blocks, 2)]
-    reach = [max(min(2 * abs(order[f]) + 1, halfz) for f, _, _ in group) for group in groups]
+    reach = [max(min(2 * abs(order[f]) + 1, halfz) for f, _ in group) for group in groups]
 
     def project(block):
         for i in range(2):
@@ -350,38 +340,58 @@
         part[:, span(block, tile)] = lax.dot_general(
             tokens[...], columns, (((1,), (1,)), ((), ())), preferred_element_type=jnp.float32)
 
-    def term(direction, block, t):
-        return part[span(away(x, -direction * t, nx), rows), span(block, tile)]
+    def term(block, ahead):
+        return part[span(away(x, ahead, nx), rows), span(block, tile)]
+
+    sides = (1, -1)
+
+    def hops(f, direction):
+        return halfx if (f % 2 == 0) == (direction > 0) else halfx - 1
 
     def rs(f, direction, t):
-        return remote(sums_out.at[f, t], sums_in.at[f, t], rs_send.at[f, t], rs_recv.at[f, t],
+        i = 2 * f + (1 if direction > 0 else 0)
+        return remote(sums_out.at[i, t], sums_in.at[i, t], rs_send.at[i, t], rs_recv.at[i, t],
                       head=away(x, direction, nx))
 
-    for turn in range(nx + len(groups) - 1):
+    def advance(group, t):
+        for direction in sides:
+            for f, block in group:
+                last = hops(f, direction)
+                if t > last:
+                    continue
+                i = 2 * f + (1 if direction > 0 else 0)
+                value = term(block, direction * (last - t + 1))
+                if t > 1:
+                    rs(f, direction, t - 1).wait_recv()
+                    value = value + sums_in[i, t - 1].astype(jnp.float32)
+                sums_out[i, t] = value.astype(jnp.bfloat16)
+                rs(f, direction, t).start()
+
+    def finish(group):
+        for f, block in group:
+            total = term(block, 0)
+            for direction in sides:
+                last = hops(f, direction)
+                if last:
+                    rs(f, direction, last).wait_recv()
+                    total = total + sums_in[2 * f + (1 if direction > 0 else 0), last].astype(jnp.float32)
+            at = span(block, tile)
+            owned[:, at] = (res[:, at].astype(jnp.float32) + gate[:, at] * total).astype(jnp.bfloat16)
+
+    entry = [max(0, g - 1) for g in range(len(groups))]
+    for load in late:
+        load.wait()
+    for turn in range(halfx + 1 + entry[-1]):
         for g, group in enumerate(groups):
-            t = turn - g + 1
+            t = turn - entry[g] + 1
             if t == 1:
                 w_reach(reach[g])
-                for f, direction, block in group:
+                for f, block in group:
                     project(block)
-                for f, direction, block in group:
-                    sums_out[f, 1] = term(direction, block, 1).astype(jnp.bfloat16)
-                for f, direction, block in group:
-                    rs(f, direction, 1).start()
-            elif 1 < t < nx:
-                for f, direction, block in group:
-                    rs(f, direction, t - 1).wait_recv()
-                    sums_out[f, t] = (sums_in[f, t - 1].astype(jnp.float32) + term(direction, block, t)).astype(jnp.bfloat16)
-                    rs(f, direction, t).start()
-            elif t == nx:
-                if g == 0:
-                    for load in late:
-                        load.wait()
-                for f, direction, block in group:
-                    rs(f, direction, nx - 1).wait_recv()
-                    total = sums_in[f, nx - 1].astype(jnp.float32) + term(direction, block, nx)
-                    at = span(block, tile)
-                    owned[:, at] = (res[:, at].astype(jnp.float32) + gate[:, at] * total).astype(jnp.bfloat16)
+            if 1 <= t <= halfx:
+                advance(group, t)
+            elif t == halfx + 1:
+                finish(group)
         w_reach(6 + turn)
 
     out = pltpu.make_async_copy(owned, hidden_ref, out_sem.at[0])
@@ -450,12 +460,10 @@
 
     lax.fori_loop(0, nz, drain_pair, 0)
 
-    def drain_rs(t, carry):
-        for f, direction, block in flows:
-            rs(f, direction, t).wait_send()
-        return carry
-
-    lax.fori_loop(1, nx, drain_rs, 0)
+    for f, block in flows:
+        for direction in sides:
+            for t in range(1, hops(f, direction) + 1):
+                rs(f, direction, t).wait_send()
     for copy, goes, comes in sends:
         @pl.when(comes)
         def _():
@@ -503,8 +511,8 @@
             pltpu.VMEM((heads, HEAD_DIM, count), f32),
             pltpu.VMEM((heads, 2, 1, count), f32),
             pltpu.VMEM((count, model), f32),
-            pltpu.VMEM((nz // 2, nx, rows, tile), bf),
-            pltpu.VMEM((nz // 2, nx, rows, tile), bf),
+            pltpu.VMEM((nz, nx // 2 + 1, rows, tile), bf),
+            pltpu.VMEM((nz, nx // 2 + 1, rows, tile), bf),
             pltpu.VMEM((count, width), bf),
             pltpu.VMEM((planes, HEAD_DIM), bf),
             pltpu.VMEM((rows, model), bf),
@@ -523,7 +531,7 @@
             dma((nz,)), dma((2 * nx,)),
             dma((2, nz // 2 + 1)), dma((2, nz // 2 + 1)),
             dma((nz,)), dma((nz,)),
-            dma((nz // 2, nx)), dma((nz // 2, nx)),
+            dma((nz, nx // 2 + 1)), dma((nz, nx // 2 + 1)),
             dma((5,)), dma((5,)), dma((1,)),
         ],
         compiler_params=pltpu.CompilerParams(

time: 175 us -> 164 us (0.937)
  Pallas kernels: 169 us -> 156 us
    pallas_call x1, Pallas kernels: 169 us -> 156 us  [transformer_part(): pl.pallas_call(functools.partial(block_kernel, nx, nz), out_shape=(jax.Sh...]
where the time goes in v5:
time: 164 us; the launch traced here: 163 us
  Pallas kernels  156 us (95%)
  local copies, waits for them, and re-layouts  4.32 us (3%)
    pallas_call x1, Pallas kernels, transformer_part(): pl.pallas_call(functools.partial(block_kernel, nx, nz), out_shape=(jax.Sh...  156 us

profile of v5, /device:TPU:65, one launch (start us, length us, event | category | flops | bytes accessed | tf_op | source)
XLA Modules:
  0.0 162.5 jit_solution(5815998875616650373)
XLA Ops:
  0.6 0.0 copy-start
  0.6 1.0 copy-done
  1.6 156.4 %block_ring.1 = (bf16[32,5120]{1,0:T(8,128)(2,1)}, bf16[2,3,32,128]{3,2,1,0:T(8,128)(2,1)}) custom-call(bf16[32,3072]{1,0:T(8,128)(2,1)} %bitcast.33, bf16[32,3072]{1,0:T(8,128)(2,1)} %bitcast.34, bf16[32,3072]{1,0:T(8,128)(2,1)} %bitcast.35, bf16[160,384]{1,0:T(8,128)(2,1)} %bitcast.36, bf16[32,5120]{1,0:T(8,128)(2,1)} %bitcast.32, f32[1,5120]{1,0:T(1,128)} %bitcast.37, ...), custom_call_target="tpu_custom_call" | custom-call | flops 3221225472 | bytes 2097152 | tf_op jit(solution)/shard_map/block_ring/pallas_call | solution.py:497
  158.0 0.9 reshape.65
  159.0 0.2 copy.16
  159.2 0.1 pad_slice_fusion
  159.3 0.0 copy-start.2
  159.4 0.3 concatenate.3
  159.7 0.3 copy-done.2
  160.0 0.0 copy-start.1
  160.0 0.3 multiply_reduce_fusion
  160.3 0.0 copy-start.3
  160.4 0.7 copy-done.3
  161.0 0.8 multiply_convert_fusion
  161.8 0.0 copy-done.1
  161.8 0.7 copy.19
  (3 shorter events, 0.1 us)
Async XLA Ops:
  0.6 1.0 copy-start
  159.3 0.7 copy-start.2
  160.0 1.8 %copy-start.1 = (bf16[32,5120]{1,0:T(8,128)(2,1)S(1)}, bf16[32,5120]{1,0:T(8,128)(2,1)}, u32[]{:S(2)}) copy-start(bf16[32,5120]{1,0:T(8,128)(2,1)} %get-tuple-element.4) | copy-start | bytes 983044
  160.3 0.7 copy-start.3

commit v6 on v5

--- a/solution.py
+++ b/solution.py
@@ -11,38 +11,13 @@
 MESH = pl.DeviceIdType.MESH
 
 
-def convolve(padded, frames, conv_weight, conv_bias, norm_gain):
-    height = padded.shape[1] - 2
-    breadth = padded.shape[2] - 2
-    stacked = jnp.concatenate(
-        [
-            padded[
-                time_off : time_off + frames,
-                row_off : row_off + height,
-                col_off : col_off + breadth,
-            ]
-            for time_off in range(3)
-            for row_off in range(3)
-            for col_off in range(3)
-        ],
-        -1,
-    )
-    kernel = conv_weight.reshape(-1, conv_weight.shape[-1])
-    linear = (
-        jnp.dot(stacked.reshape(-1, stacked.shape[-1]), kernel, preferred_element_type=jnp.float32)
-        + conv_bias
-    )
-    normed = linear * lax.rsqrt(jnp.mean(linear * linear, -1, keepdims=True) + 1e-06) * norm_gain
-    return jax.nn.silu(normed).astype(jnp.bfloat16).reshape(frames, height, breadth, -1)
-
-
-def block_kernel(nx, nz, q_in, k_in, v_in, w_in, res_in, gate_in, shift_in, scale_in, hw_in, hb_in,
-                 hidden_ref, lat_ref,
-                 qa, ka, va, qp, kp, vp, wbuf, qt, acc, stat, part, sums_out, sums_in, tokens, plane_out, owned, lat,
-                 res, gate, shift, gain, hw, hb,
+def block_kernel(nx, nz, frames, q_in, k_in, v_in, w_in, res_in, gate_in, shift_in, scale_in, hw_in, hb_in,
+                 cw_in, cb_in, ng_in, owned, feat_ref,
+                 qa, ka, va, qp, kp, vp, wbuf, qt, acc, stat, part, sums_out, sums_in, tokens, plane_out, lat, video, patches,
+                 res, gate, shift, gain, hw, hb, cw, cb, ng,
                  local_sem, a2a_send, a2a_recv, ring_send, ring_recv, pair_send, pair_recv,
                  pring_send, pring_recv, ppair_send, ppair_recv, back_send, back_recv,
-                 w_send, w_recv, wpair_send, wpair_recv, rs_send, rs_recv, halo_send, halo_recv, out_sem):
+                 w_send, w_recv, wpair_send, wpair_recv, rs_send, rs_recv, halo_send, halo_recv):
     x = lax.axis_index("head")
     s = lax.axis_index("seq")
     z, c = s // 2, lax.rem(s, 2)
@@ -79,11 +54,13 @@
     loads += [pltpu.make_async_copy(ins[i].at[:, plane_head(z)], plane_dst[i].at[span(z, rows), :], local_sem.at[3 + i])
               for i in range(3)]
     w_load = pltpu.make_async_copy(w_in, wbuf.at[z, c], local_sem.at[6])
-    late = ((res_in, res), (gate_in, gate), (shift_in, shift), (scale_in, gain), (hw_in, hw), (hb_in, hb))
+    late = ((res_in, res), (gate_in, gate), (shift_in, shift), (scale_in, gain), (hw_in, hw), (hb_in, hb),
+            (cw_in, cw), (cb_in, cb), (ng_in, ng))
     late = [pltpu.make_async_copy(a, b, local_sem.at[7 + i]) for i, (a, b) in enumerate(late)]
     for load in loads + [w_load] + late:
         load.start()
     lat[...] = jnp.zeros_like(lat)
+    video[...] = jnp.zeros_like(video)
 
     alone = (z // 2 == x).astype(jnp.int32)
     barrier = pltpu.get_barrier_semaphore()
@@ -287,9 +264,15 @@
         plane_attend(away(x, i, nx))
         col_step(2 * i + 1, (1,))
         col_attend_at(2 * i)
+        if halfx > 2:
+            @pl.when(i > halfx - 3)
+            def _():
+                w_step(i + 5 - halfx)
         return carry
 
     lax.fori_loop(1, halfx, step, 0)
+    if halfx > 2:
+        w_at[0] = 4
     w_reach(3)
     plane_attend(away(x, halfx, nx))
 
@@ -316,10 +299,10 @@
 
     col_step(halfz)
     col_attend_at(halfz - 1)
-    w_reach(4)
+    w_reach(5)
     col_attend([away(z, halfz, nz)])
     tokens[:, 0:HEAD_DIM] = (acc[0] / stat[0, 1]).T.astype(jnp.bfloat16)
-    w_reach(5)
+    w_reach(6)
     for xx in range(nx):
         for part_of in range(2):
             @pl.when(jnp.logical_or(alone == 0, jnp.logical_or(x != xx, which != part_of)))
@@ -378,7 +361,7 @@
             at = span(block, tile)
             owned[:, at] = (res[:, at].astype(jnp.float32) + gate[:, at] * total).astype(jnp.bfloat16)
 
-    entry = [max(0, g - 1) for g in range(len(groups))]
+    entry = [g // 2 for g in range(len(groups))]
     for load in late:
         load.wait()
     for turn in range(halfx + 1 + entry[-1]):
@@ -392,10 +375,8 @@
                 advance(group, t)
             elif t == halfx + 1:
                 finish(group)
-        w_reach(6 + turn)
-
-    out = pltpu.make_async_copy(owned, hidden_ref, out_sem.at[0])
-    out.start()
+        w_reach(7 + turn)
+
     values = owned[...].astype(jnp.float32)
     center = values - jnp.mean(values, -1, keepdims=True)
     spread = jnp.mean(center * center, -1, keepdims=True)
@@ -468,16 +449,34 @@
         @pl.when(comes)
         def _():
             copy().wait_recv()
-    lat_ref[...] = lat[...]
+    channels, breadth = cells // 4, rows // frames
+    for group_of in range(2):
+        for frame in range(frames):
+            here = slice(frame * breadth, (frame + 1) * breadth)
+            for line, (row, a) in enumerate(((0, 1), (1, 0), (1, 1), (2, 0))):
+                for b in range(2):
+                    at = (2 * a + b) * channels
+                    video[group_of * frames + frame, line, pl.ds(1 + b, breadth, stride=2), :] = (
+                        lat[group_of, row, here, at:at + channels].astype(jnp.float32))
+    for k in range(27):
+        dt, dy, dx = k // 9, k // 3 % 3, k % 3
+        for frame in range(frames):
+            for line in range(2):
+                at = (2 * frame + line) * 2 * breadth
+                patches[at:at + 2 * breadth, k * channels:(k + 1) * channels] = (
+                    video[frame + dt, line + dy, dx:dx + 2 * breadth, :])
+    linear = jnp.dot(patches[...].astype(jnp.bfloat16), cw[...], preferred_element_type=jnp.float32) + cb[...]
+    level = lax.rsqrt(jnp.mean(linear * linear, -1, keepdims=True) + 1e-06)
+    gated = linear * level * ng[...]
+    feat_ref[...] = (gated / (1.0 + jnp.exp(-gated))).astype(feat_ref.dtype)
     for copy, goes, comes in sends:
         @pl.when(goes)
         def _():
             copy().wait_send()
-    out.wait()
 
 
 def transformer_part(queries, attn_keys, attn_values, residual, out_weight, out_gate,
-                     head_shift, head_scale, head_weight, head_bias):
+                     head_shift, head_scale, head_weight, head_bias, conv_weight, conv_bias, norm_gain):
     nx, nz = lax.axis_size("head"), lax.axis_size("seq") // 2
     frames, height, breadth, features = queries.shape
     model = residual.shape[3]
@@ -489,16 +488,20 @@
     if nz != 2 * nx or heads != 3:
         raise ValueError("unsupported mesh")
     cells = head_weight.shape[1]
+    taps, outs = conv_weight.size // conv_weight.shape[-1], conv_weight.shape[-1]
+    places = 4 * rows
+    if frames != 2 or conv_weight.shape[:3] != (3, 3, 3) or height != 1:
+        raise ValueError("unsupported shape")
     there = pl.BlockSpec(memory_space=pltpu.HBM)
     vmem = pl.BlockSpec(memory_space=pltpu.VMEM)
     dma = pltpu.SemaphoreType.DMA
     bf, f32 = jnp.bfloat16, jnp.float32
     tile = 4 * share_cols
     return pl.pallas_call(
-        functools.partial(block_kernel, nx, nz),
-        out_shape=(jax.ShapeDtypeStruct((rows, model), bf), jax.ShapeDtypeStruct((2, 3, rows, 2 * cells), bf)),
-        in_specs=[there] * 10,
-        out_specs=(there, vmem),
+        functools.partial(block_kernel, nx, nz, frames),
+        out_shape=(jax.ShapeDtypeStruct((rows, model), bf), jax.ShapeDtypeStruct((places, outs), bf)),
+        in_specs=[there] * 13,
+        out_specs=(vmem, vmem),
         scratch_shapes=[
             pltpu.VMEM((count, HEAD_DIM), bf),
             pltpu.VMEM((2, nz, count, HEAD_DIM), bf),
@@ -515,15 +518,19 @@
             pltpu.VMEM((nz, nx // 2 + 1, rows, tile), bf),
             pltpu.VMEM((count, width), bf),
             pltpu.VMEM((planes, HEAD_DIM), bf),
-            pltpu.VMEM((rows, model), bf),
             pltpu.VMEM((2, 3, rows, 2 * cells), bf),
+            pltpu.VMEM((2 * frames, 4, 2 * breadth + 8, cells // 4), f32),
+            pltpu.VMEM((places, taps), f32),
             pltpu.VMEM((rows, model), bf),
             pltpu.VMEM((1, model), f32),
             pltpu.VMEM((1, model), f32),
             pltpu.VMEM((1, model), f32),
             pltpu.VMEM((cells, model), bf),
             pltpu.VMEM((1, cells), f32),
-            dma((13,)), dma((6,)), dma((6,)),
+            pltpu.VMEM((taps, outs), bf),
+            pltpu.VMEM((1, outs), f32),
+            pltpu.VMEM((1, outs), f32),
+            dma((16,)), dma((6,)), dma((6,)),
             dma((4, nz // 2 + 1)), dma((4, nz // 2 + 1)),
             dma((2, nz)), dma((2, nz)),
             dma((4, nx // 2 + 1)), dma((4, nx // 2 + 1)),
@@ -532,7 +539,7 @@
             dma((2, nz // 2 + 1)), dma((2, nz // 2 + 1)),
             dma((nz,)), dma((nz,)),
             dma((nz, nx // 2 + 1)), dma((nz, nx // 2 + 1)),
-            dma((5,)), dma((5,)), dma((1,)),
+            dma((5,)), dma((5,)),
         ],
         compiler_params=pltpu.CompilerParams(
             collective_id=0, has_side_effects=True, vmem_limit_bytes=56 * 2**20),
@@ -540,20 +547,16 @@
         name="block_ring",
     )(queries.reshape(rows, features), attn_keys.reshape(rows, features), attn_values.reshape(rows, features),
       out_weight.T, residual.reshape(rows, model), out_gate.reshape(1, model), head_shift.reshape(1, model),
-      head_scale.reshape(1, model), head_weight.T, head_bias.reshape(1, cells))
+      head_scale.reshape(1, model), head_weight.T, head_bias.reshape(1, cells),
+      conv_weight.reshape(taps, outs), conv_bias.reshape(1, outs), norm_gain.reshape(1, outs))
 
 
 def on_device(queries, attn_keys, attn_values, residual, out_weight, out_gate, head_shift, head_scale,
               head_weight, head_bias, conv_weight, conv_bias, norm_gain):
     frames, height, breadth = queries.shape[:3]
-    channels = head_weight.shape[1] // 4
-    hidden, lat = transformer_part(queries, attn_keys, attn_values, residual, out_weight, out_gate,
-                                   head_shift, head_scale, head_weight, head_bias)
-    cells = lat[..., : 4 * channels].reshape(2, 3, frames, breadth, 2, 2, channels)
-    video = cells.transpose(0, 2, 1, 4, 3, 5, 6).reshape(2 * frames, 6, 2 * breadth, channels)[:, 1:5]
-    padded = jnp.pad(video, ((0, 0), (0, 0), (1, 1), (0, 0)))
-    features = convolve(padded, frames, conv_weight, conv_bias, norm_gain)
-    return hidden.reshape(residual.shape), features
+    hidden, features = transformer_part(queries, attn_keys, attn_values, residual, out_weight, out_gate, head_shift,
+                                        head_scale, head_weight, head_bias, conv_weight, conv_bias, norm_gain)
+    return hidden.reshape(residual.shape), features.reshape(frames, 2 * height, 2 * breadth, -1)
 
 
 def solution(mesh):

time: 164 us -> 161 us (0.982)
  no operation moved by 1% of the time
where the time goes in v6:
time: 161 us
  Pallas kernels  156 us (97%)
  local copies, waits for them, and re-layouts  4.32 us (3%)
    pallas_call x1, Pallas kernels, transformer_part(): pl.pallas_call(functools.partial(block_kernel, nx, nz, frames), out_shape...  156 us

profile of v6, /device:TPU:65, one launch (start us, length us, event | category | flops | bytes accessed | tf_op | source)
XLA Modules:
  0.0 161.0 jit_solution(7991095099753154769)
XLA Ops:
  0.6 0.0 copy-start.1
  0.6 0.7 copy-done.1
  1.3 0.0 copy-start.2
  1.3 0.6 reshape.52.cb_in
  1.9 0.1 copy-done.2
  2.0 0.6 reshape.53.ng_in
  2.6 156.1 %block_ring.1 = (bf16[32,5120]{1,0:T(8,128)(2,1)}, bf16[128,384]{1,0:T(8,128)(2,1)}) custom-call(bf16[32,3072]{1,0:T(8,128)(2,1)} %bitcast.20, bf16[32,3072]{1,0:T(8,128)(2,1)} %bitcast.21, bf16[32,3072]{1,0:T(8,128)(2,1)} %bitcast.22, bf16[160,384]{1,0:T(8,128)(2,1)} %bitcast.23, bf16[32,5120]{1,0:T(8,128)(2,1)} %bitcast.19, f32[1,5120]{1,0:T(1,128)} %bitcast.24, ...), custom_call_target="tpu_custom_call" | custom-call | flops 3221225472 | bytes 2097152 | tf_op jit(solution)/shard_map/block_ring/pallas_call | solution.py:500
  158.6 0.0 copy-start
  158.6 1.8 %copy.18 = bf16[2,1,16,5120]{3,2,1,0:T(8,128)(2,1)} copy(bf16[2,1,16,5120]{3,2,1,0:T(8,128)(2,1)} %bitcast.15) | data formatting | bytes 655360
  160.4 0.0 copy-done
  160.4 0.6 copy.19
Async XLA Ops:
  0.6 0.7 copy-start.1
  1.3 0.7 copy-start.2
  158.6 1.8 %copy-start = (bf16[128,384]{1,0:T(8,128)(2,1)S(1)}, bf16[128,384]{1,0:T(8,128)(2,1)}, u32[]{:S(2)}) copy-start(bf16[128,384]{1,0:T(8,128)(2,1)} %get-tuple-element.5) | copy-start | bytes 294916

commit v7 on v6

--- a/solution.py
+++ b/solution.py
@@ -12,12 +12,12 @@
 
 
 def block_kernel(nx, nz, frames, q_in, k_in, v_in, w_in, res_in, gate_in, shift_in, scale_in, hw_in, hb_in,
-                 cw_in, cb_in, ng_in, owned, feat_ref,
-                 qa, ka, va, qp, kp, vp, wbuf, qt, acc, stat, part, sums_out, sums_in, tokens, plane_out, lat, video, patches,
+                 cw_in, cb_in, ng_in, hidden_ref, feat_ref,
+                 qa, ka, va, qp, kp, vp, wbuf, qt, acc, stat, part, sums_out, sums_in, tokens, plane_out, owned, feat, lat, video, patches,
                  res, gate, shift, gain, hw, hb, cw, cb, ng,
                  local_sem, a2a_send, a2a_recv, ring_send, ring_recv, pair_send, pair_recv,
                  pring_send, pring_recv, ppair_send, ppair_recv, back_send, back_recv,
-                 w_send, w_recv, wpair_send, wpair_recv, rs_send, rs_recv, halo_send, halo_recv):
+                 w_send, w_recv, wpair_send, wpair_recv, rs_send, rs_recv, halo_send, halo_recv, out_sem):
     x = lax.axis_index("head")
     s = lax.axis_index("seq")
     z, c = s // 2, lax.rem(s, 2)
@@ -115,27 +115,27 @@
 
     def hop(kv, direction, step, back):
         slot, flow = col_kv[kv].at[c, away(z, -direction * back, nz)], flow_of(kv, direction)
-        return remote(slot, slot, ring_send.at[flow, step], ring_recv.at[flow, step], seq=seq_of(z + direction, c))
+        return remote(slot, slot, ring_send.at[kv], ring_recv.at[flow, step - 1], seq=seq_of(z + direction, c))
 
     def share(kv, zz, cc):
         slot = col_kv[kv].at[cc, zz]
-        return remote(slot, slot, pair_send.at[kv, zz], pair_recv.at[kv, zz], seq=seq_of(z, 1 - c))
+        return remote(slot, slot, pair_send.at[kv], pair_recv.at[kv, zz], seq=seq_of(z, 1 - c))
 
     def phop(kv, direction, step, back):
         slot, flow = plane_kv[kv].at[c, away(x, -direction * back, nx)], flow_of(kv, direction)
-        return remote(slot, slot, pring_send.at[flow, step], pring_recv.at[flow, step], head=away(x, direction, nx))
+        return remote(slot, slot, pring_send.at[kv], pring_recv.at[flow, step - 1], head=away(x, direction, nx))
 
     def pshare(kv, xx, cc):
         slot = plane_kv[kv].at[cc, xx]
-        return remote(slot, slot, ppair_send.at[kv, xx], ppair_recv.at[kv, xx], seq=seq_of(z, 1 - c))
+        return remote(slot, slot, ppair_send.at[kv], ppair_recv.at[kv, xx], seq=seq_of(z, 1 - c))
 
     def w_hop(direction, step, back):
         slot, flow = wbuf.at[away(z, -direction * back, nz), c], 1 if direction > 0 else 0
-        return remote(slot, slot, w_send.at[flow, step], w_recv.at[flow, step], seq=seq_of(z + direction, c))
+        return remote(slot, slot, w_send.at[0], w_recv.at[flow, step - 1], seq=seq_of(z + direction, c))
 
     def w_share(zz, cc):
         slot = wbuf.at[zz, cc]
-        return remote(slot, slot, wpair_send.at[zz], wpair_recv.at[zz], seq=seq_of(z, 1 - c))
+        return remote(slot, slot, wpair_send.at[0], wpair_recv.at[zz], seq=seq_of(z, 1 - c))
 
     def last_hop(kv, direction, half):
         return half if (kv == 0) == (direction > 0) else half - 1
@@ -282,7 +282,7 @@
 
     def back(zz, xx, part_of):
         return remote(plane_out.at[span(zz, rows), :], tokens.at[span(xx, rows), span(1 + part_of, HEAD_DIM)],
-                      back_send.at[zz], back_recv.at[2 * xx + part_of], head=group, seq=seq_of(zz, c))
+                      back_send.at[0], back_recv.at[2 * xx + part_of], head=group, seq=seq_of(zz, c))
 
     for d in far_first(nz) + [0]:
         zz = away(z, d, nz)
@@ -331,10 +331,12 @@
     def hops(f, direction):
         return halfx if (f % 2 == 0) == (direction > 0) else halfx - 1
 
+    def slot_of(f, direction, t):
+        return f * (nx - 1) + (0 if direction > 0 else hops(f, 1)) + t - 1
+
     def rs(f, direction, t):
-        i = 2 * f + (1 if direction > 0 else 0)
-        return remote(sums_out.at[i, t], sums_in.at[i, t], rs_send.at[i, t], rs_recv.at[i, t],
-                      head=away(x, direction, nx))
+        i = slot_of(f, direction, t)
+        return remote(sums_out.at[i], sums_in.at[i], rs_send.at[0], rs_recv.at[i], head=away(x, direction, nx))
 
     def advance(group, t):
         for direction in sides:
@@ -342,12 +344,11 @@
                 last = hops(f, direction)
                 if t > last:
                     continue
-                i = 2 * f + (1 if direction > 0 else 0)
                 value = term(block, direction * (last - t + 1))
                 if t > 1:
                     rs(f, direction, t - 1).wait_recv()
-                    value = value + sums_in[i, t - 1].astype(jnp.float32)
-                sums_out[i, t] = value.astype(jnp.bfloat16)
+                    value = value + sums_in[slot_of(f, direction, t - 1)].astype(jnp.float32)
+                sums_out[slot_of(f, direction, t)] = value.astype(jnp.bfloat16)
                 rs(f, direction, t).start()
 
     def finish(group):
@@ -357,7 +358,7 @@
                 last = hops(f, direction)
                 if last:
                     rs(f, direction, last).wait_recv()
-                    total = total + sums_in[2 * f + (1 if direction > 0 else 0), last].astype(jnp.float32)
+                    total = total + sums_in[slot_of(f, direction, last)].astype(jnp.float32)
             at = span(block, tile)
             owned[:, at] = (res[:, at].astype(jnp.float32) + gate[:, at] * total).astype(jnp.bfloat16)
 
@@ -377,6 +378,8 @@
                 finish(group)
         w_reach(7 + turn)
 
+    out = pltpu.make_async_copy(owned, hidden_ref, out_sem.at[0])
+    out.start()
     values = owned[...].astype(jnp.float32)
     center = values - jnp.mean(values, -1, keepdims=True)
     spread = jnp.mean(center * center, -1, keepdims=True)
@@ -407,44 +410,26 @@
         from_column(i).wait_send()
         from_plane(i).wait_send()
 
-    def drain(h, carry):
-        for kv in range(2):
-            for direction in (1, -1):
-                @pl.when(h <= last_hop(kv, direction, halfz))
-                def _():
-                    hop(kv, direction, h, h - 1).wait_send()
-
-                @pl.when(h <= last_hop(kv, direction, halfx))
-                def _():
-                    phop(kv, direction, h, h - 1).wait_send()
-        for direction in (1, -1):
-            @pl.when(h <= w_last(direction))
-            def _():
-                w_hop(direction, h, h - 1).wait_send()
-        return carry
-
-    lax.fori_loop(1, halfz + 1, drain, 0)
-
-    def drain_pair(zz, carry):
-        for kv in range(2):
-            share(kv, zz, c).wait_send()
-
-            @pl.when(zz < nx)
-            def _():
-                pshare(kv, zz, c).wait_send()
-        w_share(zz, c).wait_send()
-
-        @pl.when(jnp.logical_or(alone == 0, zz != z))
-        def _():
-            back(zz, x, which).wait_send()
-        return carry
-
-    lax.fori_loop(0, nz, drain_pair, 0)
-
-    for f, block in flows:
-        for direction in sides:
-            for t in range(1, hops(f, direction) + 1):
-                rs(f, direction, t).wait_send()
+    def sent(ref, sem):
+        remote(ref, ref, sem, sem, head=away(x, 1, nx)).wait_send()
+
+    for kv in range(2):
+        sent(col_kv[kv].at[0, pl.ds(0, nz - 1)], ring_send.at[kv])
+        sent(col_kv[kv].at[0], pair_send.at[kv])
+        sent(plane_kv[kv].at[0, pl.ds(0, nx - 1)], pring_send.at[kv])
+        sent(plane_kv[kv].at[0], ppair_send.at[kv])
+    sent(wbuf.at[pl.ds(0, nz - 1), 0], w_send.at[0])
+    sent(wbuf.at[:, 0], wpair_send.at[0])
+    sent(sums_out, rs_send.at[0])
+
+    @pl.when(alone == 0)
+    def _():
+        sent(plane_out, back_send.at[0])
+
+    @pl.when(alone == 1)
+    def _():
+        sent(plane_out.at[pl.ds(0, rows * (nz - 1)), :], back_send.at[0])
+
     for copy, goes, comes in sends:
         @pl.when(comes)
         def _():
@@ -465,14 +450,18 @@
                 at = (2 * frame + line) * 2 * breadth
                 patches[at:at + 2 * breadth, k * channels:(k + 1) * channels] = (
                     video[frame + dt, line + dy, dx:dx + 2 * breadth, :])
-    linear = jnp.dot(patches[...].astype(jnp.bfloat16), cw[...], preferred_element_type=jnp.float32) + cb[...]
+    linear = jnp.dot(patches[...].astype(jnp.bfloat16), cw[...], preferred_element_type=jnp.float32) + cb[...][None, :]
     level = lax.rsqrt(jnp.mean(linear * linear, -1, keepdims=True) + 1e-06)
-    gated = linear * level * ng[...]
-    feat_ref[...] = (gated / (1.0 + jnp.exp(-gated))).astype(feat_ref.dtype)
+    gated = linear * level * ng[...][None, :]
+    feat[...] = (gated / (1.0 + jnp.exp(-gated))).astype(feat.dtype)
+    feat_out = pltpu.make_async_copy(feat, feat_ref, out_sem.at[1])
+    feat_out.start()
     for copy, goes, comes in sends:
         @pl.when(goes)
         def _():
             copy().wait_send()
+    out.wait()
+    feat_out.wait()
 
 
 def transformer_part(queries, attn_keys, attn_values, residual, out_weight, out_gate,
@@ -493,7 +482,6 @@
     if frames != 2 or conv_weight.shape[:3] != (3, 3, 3) or height != 1:
         raise ValueError("unsupported shape")
     there = pl.BlockSpec(memory_space=pltpu.HBM)
-    vmem = pl.BlockSpec(memory_space=pltpu.VMEM)
     dma = pltpu.SemaphoreType.DMA
     bf, f32 = jnp.bfloat16, jnp.float32
     tile = 4 * share_cols
@@ -501,7 +489,7 @@
         functools.partial(block_kernel, nx, nz, frames),
         out_shape=(jax.ShapeDtypeStruct((rows, model), bf), jax.ShapeDtypeStruct((places, outs), bf)),
         in_specs=[there] * 13,
-        out_specs=(vmem, vmem),
+        out_specs=(there, there),
         scratch_shapes=[
             pltpu.VMEM((count, HEAD_DIM), bf),
             pltpu.VMEM((2, nz, count, HEAD_DIM), bf),
@@ -514,10 +502,12 @@
             pltpu.VMEM((heads, HEAD_DIM, count), f32),
             pltpu.VMEM((heads, 2, 1, count), f32),
             pltpu.VMEM((count, model), f32),
-            pltpu.VMEM((nz, nx // 2 + 1, rows, tile), bf),
-            pltpu.VMEM((nz, nx // 2 + 1, rows, tile), bf),
+            pltpu.VMEM((nz // 2 * (nx - 1), rows, tile), bf),
+            pltpu.VMEM((nz // 2 * (nx - 1), rows, tile), bf),
             pltpu.VMEM((count, width), bf),
             pltpu.VMEM((planes, HEAD_DIM), bf),
+            pltpu.VMEM((rows, model), bf),
+            pltpu.VMEM((places, outs), bf),
             pltpu.VMEM((2, 3, rows, 2 * cells), bf),
             pltpu.VMEM((2 * frames, 4, 2 * breadth + 8, cells // 4), f32),
             pltpu.VMEM((places, taps), f32),
@@ -528,18 +518,15 @@
             pltpu.VMEM((cells, model), bf),
             pltpu.VMEM((1, cells), f32),
             pltpu.VMEM((taps, outs), bf),
-            pltpu.VMEM((1, outs), f32),
-            pltpu.VMEM((1, outs), f32),
+            pltpu.VMEM((outs,), f32),
+            pltpu.VMEM((outs,), f32),
             dma((16,)), dma((6,)), dma((6,)),
-            dma((4, nz // 2 + 1)), dma((4, nz // 2 + 1)),
-            dma((2, nz)), dma((2, nz)),
-            dma((4, nx // 2 + 1)), dma((4, nx // 2 + 1)),
-            dma((2, nx)), dma((2, nx)),
-            dma((nz,)), dma((2 * nx,)),
-            dma((2, nz // 2 + 1)), dma((2, nz // 2 + 1)),
-            dma((nz,)), dma((nz,)),
-            dma((nz, nx // 2 + 1)), dma((nz, nx // 2 + 1)),
-            dma((5,)), dma((5,)),
+            dma((2,)), dma((4, nz // 2)), dma((2,)), dma((2, nz)),
+            dma((2,)), dma((4, nx // 2)), dma((2,)), dma((2, nx)),
+            dma((1,)), dma((2 * nx,)),
+            dma((1,)), dma((2, nz // 2)), dma((1,)), dma((nz,)),
+            dma((1,)), dma((nz // 2 * (nx - 1),)),
+            dma((5,)), dma((5,)), dma((2,)),
         ],
         compiler_params=pltpu.CompilerParams(
             collective_id=0, has_side_effects=True, vmem_limit_bytes=56 * 2**20),
@@ -548,7 +535,26 @@
     )(queries.reshape(rows, features), attn_keys.reshape(rows, features), attn_values.reshape(rows, features),
       out_weight.T, residual.reshape(rows, model), out_gate.reshape(1, model), head_shift.reshape(1, model),
       head_scale.reshape(1, model), head_weight.T, head_bias.reshape(1, cells),
-      conv_weight.reshape(taps, outs), conv_bias.reshape(1, outs), norm_gain.reshape(1, outs))
+      conv_weight.reshape(taps, outs), conv_bias, norm_gain)
+
+
+def deliver_kernel(a_ref, b_ref, a_out, b_out, sem):
+    copies = [pltpu.make_async_copy(a_ref, a_out, sem.at[0]), pltpu.make_async_copy(b_ref, b_out, sem.at[1])]
+    for copy in copies:
+        copy.start()
+    for copy in copies:
+        copy.wait()
+
+
+def deliver(a, b):
+    return pl.pallas_call(
+        deliver_kernel,
+        out_shape=(jax.ShapeDtypeStruct(a.shape, a.dtype), jax.ShapeDtypeStruct(b.shape, b.dtype)),
+        in_specs=[pl.BlockSpec(memory_space=pltpu.VMEM)] * 2,
+        out_specs=[pl.BlockSpec(memory_space=pltpu.HBM)] * 2,
+        scratch_shapes=[pltpu.SemaphoreType.DMA((2,))],
+        name="deliver",
+    )(a, b)
 
 
 def on_device(queries, attn_keys, attn_values, residual, out_weight, out_gate, head_shift, head_scale,
@@ -556,6 +562,7 @@
     frames, height, breadth = queries.shape[:3]
     hidden, features = transformer_part(queries, attn_keys, attn_values, residual, out_weight, out_gate, head_shift,
                                         head_scale, head_weight, head_bias, conv_weight, conv_bias, norm_gain)
+    hidden, features = deliver(hidden, features)
     return hidden.reshape(residual.shape), features.reshape(frames, 2 * height, 2 * breadth, -1)
 
 

time: 161 us -> 156 us (0.969)
  local copies, waits for them, and re-layouts: 4.32 us -> 0 us
    unnamed x8 -> x0, local copies, waits for them, and re-layouts: 3.19 us -> none
    pallas_call x1, Pallas kernels: 156 us -> 154 us  [transformer_part(): pl.pallas_call(functools.partial(block_kernel, nx, nz, frames), out_shape...]
    pallas_call x0 -> x1, Pallas kernels: none -> 1.76 us  [deliver(): pl.pallas_call(deliver_kernel, out_shape=(jax.ShapeDtypeStruct(a.shape, a...]
where the time goes in v7:
time: 156 us
  Pallas kernels  155 us (99%)
    pallas_call x1, Pallas kernels, transformer_part(): pl.pallas_call(functools.partial(block_kernel, nx, nz, frames), out_shape...  154 us

profile of v7, /device:TPU:65, one launch (start us, length us, event | category | flops | bytes accessed | tf_op | source)
XLA Modules:
  0.0 156.1 jit_solution(13556092175624136599)
XLA Ops:
  0.6 153.5 %block_ring.1 = (bf16[32,5120]{1,0:T(8,128)(2,1)}, bf16[128,384]{1,0:T(8,128)(2,1)}) custom-call(bf16[32,3072]{1,0:T(8,128)(2,1)} %bitcast.19, bf16[32,3072]{1,0:T(8,128)(2,1)} %bitcast.20, bf16[32,3072]{1,0:T(8,128)(2,1)} %bitcast.21, bf16[160,384]{1,0:T(8,128)(2,1)} %bitcast.22, bf16[32,5120]{1,0:T(8,128)(2,1)} %bitcast.17, f32[1,5120]{1,0:T(1,128)} %bitcast.24, ...), custom_call_target="tpu_custom_call" | custom-call | flops 3221225472 | bytes 2097152 | tf_op jit(solution)/shard_map/block_ring/pallas_call | solution.py:488
  154.2 1.8 %deliver.1 = (bf16[32,5120]{1,0:T(8,128)(2,1)}, bf16[128,384]{1,0:T(8,128)(2,1)}) custom-call(bf16[32,5120]{1,0:T(8,128)(2,1)} %get-tuple-element.6.a_ref, bf16[128,384]{1,0:T(8,128)(2,1)} %get-tuple-element.7.b_ref), custom_call_target="tpu_custom_call" | custom-call | tf_op jit(solution)/shard_map/deliver/pallas_call | solution.py:550

commit v8 on v7

--- a/solution.py
+++ b/solution.py
@@ -264,15 +264,11 @@
         plane_attend(away(x, i, nx))
         col_step(2 * i + 1, (1,))
         col_attend_at(2 * i)
-        if halfx > 2:
-            @pl.when(i > halfx - 3)
-            def _():
-                w_step(i + 5 - halfx)
+        w_step(i + 2)
         return carry
 
     lax.fori_loop(1, halfx, step, 0)
-    if halfx > 2:
-        w_at[0] = 4
+    w_at[0] = max(2, halfx + 1)
     w_reach(3)
     plane_attend(away(x, halfx, nx))
 
@@ -299,10 +295,10 @@
 
     col_step(halfz)
     col_attend_at(halfz - 1)
-    w_reach(5)
+    w_reach(6)
     col_attend([away(z, halfz, nz)])
     tokens[:, 0:HEAD_DIM] = (acc[0] / stat[0, 1]).T.astype(jnp.bfloat16)
-    w_reach(6)
+    w_reach(7)
     for xx in range(nx):
         for part_of in range(2):
             @pl.when(jnp.logical_or(alone == 0, jnp.logical_or(x != xx, which != part_of)))
@@ -362,7 +358,7 @@
             at = span(block, tile)
             owned[:, at] = (res[:, at].astype(jnp.float32) + gate[:, at] * total).astype(jnp.bfloat16)
 
-    entry = [g // 2 for g in range(len(groups))]
+    entry = [max(0, g - 2) for g in range(len(groups))]
     for load in late:
         load.wait()
     for turn in range(halfx + 1 + entry[-1]):
@@ -376,7 +372,7 @@
                 advance(group, t)
             elif t == halfx + 1:
                 finish(group)
-        w_reach(7 + turn)
+        w_reach(8 + turn)
 
     out = pltpu.make_async_copy(owned, hidden_ref, out_sem.at[0])
     out.start()

time: 156 us -> 157 us (level)
  no operation moved by 1% of the time
where the time goes in v8:
time: 157 us
  Pallas kernels  156 us (99%)
    pallas_call x1, Pallas kernels, transformer_part(): pl.pallas_call(functools.partial(block_kernel, nx, nz, frames), out_shape...  154 us

profile of v8, /device:TPU:65, one launch (start us, length us, event | category | flops | bytes accessed | tf_op | source)
XLA Modules:
  0.0 156.9 jit_solution(11223326275990678379)
XLA Ops:
  0.6 154.3 %block_ring.1 = (bf16[32,5120]{1,0:T(8,128)(2,1)}, bf16[128,384]{1,0:T(8,128)(2,1)}) custom-call(bf16[32,3072]{1,0:T(8,128)(2,1)} %bitcast.19, bf16[32,3072]{1,0:T(8,128)(2,1)} %bitcast.20, bf16[32,3072]{1,0:T(8,128)(2,1)} %bitcast.21, bf16[160,384]{1,0:T(8,128)(2,1)} %bitcast.22, bf16[32,5120]{1,0:T(8,128)(2,1)} %bitcast.17, f32[1,5120]{1,0:T(1,128)} %bitcast.24, ...), custom_call_target="tpu_custom_call" | custom-call | flops 3221225472 | bytes 2097152 | tf_op jit(solution)/shard_map/block_ring/pallas_call | solution.py:484
  154.9 1.8 %deliver.1 = (bf16[32,5120]{1,0:T(8,128)(2,1)}, bf16[128,384]{1,0:T(8,128)(2,1)}) custom-call(bf16[32,5120]{1,0:T(8,128)(2,1)} %get-tuple-element.6.a_ref, bf16[128,384]{1,0:T(8,128)(2,1)} %get-tuple-element.7.b_ref), custom_call_target="tpu_custom_call" | custom-call | tf_op jit(solution)/shard_map/deliver/pallas_call | solution.py:546
